TPU v7x, 256 devices: a whole 4x4x8 slice. The times are simulated.
256 devices in a mesh: blk: 64 (over z, y_hi, x), deg: 4 (over y_lo, core).
Axes of the slice: x: 4, y: 4 (y_hi: 2, y_lo: 2; y = y_hi * 2 + y_lo), z: 8, core: 2. Of those that a mesh axis runs over, the one named last changes fastest.
Arguments:
- source: bfloat16 [672, 16384], P('deg', 'blk'), may hold values from -6 to 6
- operators: bfloat16 [12, 672, 672], replicated, may hold values from -0.125 to 0.125
- mie_factor: float32 [672, 16384], P('deg', 'blk'), may hold values from 0.3 to 1.5
- pair_source: int32 [6, 4, 16384], P(None, None, 'blk'), may hold values from 0 to 255
- pair_class: int32 [6, 4, 16384], P(None, None, 'blk'), may hold values from 0 to 11
- pair_scale: bfloat16 [6, 4, 16384], P(None, None, 'blk'), may hold values from 0.25 to 1
Outputs:
- result: float32 [672, 16384], P('deg', 'blk')
Inputs may be any that keep to these rules, and one draw needn't show every extreme that they name: `pair_source`: index of a source sphere within the visited block.
All inputs are finite; a program needn't handle non-finite values.
Results may differ from a plain program's by a relative error of at most 0.0075.
Values may be sent and summed in bfloat16 or wider, within the bound.
No kernel may reach another device: no remote copies, remote signals or barrier semaphores. Data moves between devices by JAX's collectives and lax.ppermute only.
A program may use at most 64 MiB of HBM per device.

v0:
```python
import jax
import jax.numpy as jnp
from jax import lax
from jax.sharding import PartitionSpec as P


def from_behind(value, axis, steps):
    count = lax.axis_size(axis)
    pairs = [(source, (source + steps) % count) for source in range(count)]
    return lax.ppermute(value, axis, pairs)


def cut_along(x, dim, size):
    shape = x.shape
    tiles = x.reshape(*shape[:dim], size, shape[dim] // size, *shape[dim + 1 :])
    return jnp.moveaxis(tiles, dim, 0)


def summed_on_arrival(x, axis, dim):
    size = lax.axis_size(axis)
    tiles = lax.all_to_all(cut_along(x, dim, size), axis, 0, 0, tiled=True)
    return jnp.sum(tiles.astype(jnp.float32), axis=0)


def selection(indices, kinds, scales, classes, sphere_count):
    sphere_iota = jnp.arange(sphere_count, dtype=jnp.int32)[:, None, None]
    class_iota = jnp.arange(classes, dtype=jnp.int32)[None, :, None]
    table = jnp.zeros((sphere_count, classes, indices.shape[1]), jnp.float32)
    for slot in range(indices.shape[0]):
        hit = (indices[slot][None, None, :] == sphere_iota) & (
            kinds[slot][None, None, :] == class_iota
        )
        table = table + jnp.where(hit, scales[slot].astype(jnp.float32)[None, None, :], 0.0)
    return table.astype(jnp.bfloat16).reshape(sphere_count, classes * indices.shape[1])


def combine(visiting, table, classes):
    mixed = jnp.dot(visiting, table, preferred_element_type=jnp.float32)
    return mixed.astype(jnp.bfloat16).reshape(visiting.shape[0], classes, visiting.shape[1])


def local(source, operators, mie_factor, pair_source, pair_class, pair_scale):
    local_rows = source.shape[0]
    sphere_count = source.shape[1]
    classes = operators.shape[0]
    full_width = operators.shape[1]
    step_count = pair_source.shape[0]
    offset_start = lax.axis_index("deg") * local_rows
    weight_cols = lax.dynamic_slice_in_dim(operators, offset_start, local_rows, 2)
    weight_flat = jnp.transpose(weight_cols, (1, 2, 0)).reshape(full_width, local_rows * classes)
    target_field = jnp.zeros((full_width, sphere_count), jnp.float32)
    visiting = source
    for cycle_step in range(step_count):
        if cycle_step > 0:
            visiting = from_behind(source, "blk", cycle_step)
        table = selection(
            pair_source[cycle_step],
            pair_class[cycle_step],
            pair_scale[cycle_step],
            classes,
            sphere_count,
        )
        combined = combine(visiting, table, classes)
        operand = combined.reshape(combined.shape[0] * classes, sphere_count)
        target_field = target_field + jnp.dot(
            weight_flat, operand, preferred_element_type=jnp.float32
        )
    target_field = summed_on_arrival(target_field.astype(jnp.bfloat16), "deg", 0)
    return source.astype(jnp.float32) - mie_factor * target_field


def solution(mesh):
    return jax.shard_map(
        local,
        mesh=mesh,
        in_specs=(
            P("deg", "blk"),
            P(),
            P("deg", "blk"),
            P(None, None, "blk"),
            P(None, None, "blk"),
            P(None, None, "blk"),
        ),
        out_specs=P("deg", "blk"),
        check_vma=False,
    )
```

profile of v0, /device:TPU:69, one launch (start us, length us, event | category | flops | bytes accessed | tf_op | source)
XLA Modules:
  0.0 106.7 jit_solution(17746635082022495456)
XLA Ops:
  0.0 0.9 collective-permute-start
  0.9 3.2 %collective-permute-start.1 = (bf16[168,256]{1,0:T(8,128)(2,1)}, bf16[168,256]{1,0:T(8,128)(2,1)S(1)}, u32[]{:S(2)}, u32[]{:S(2)}) collective-permute-start(bf16[168,256]{1,0:T(8,128)(2,1)} %param.6), channel_id=1, source_target_pairs={{0,8},{4,12},{8,16},{12,20},{16,24},{20,28},{24,32},{28,36},{32,40... | collective-permute-start | bytes 258056 | tf_op jit(solution)/shard_map/ppermute | solution.py:10
  4.1 2.0 %collective-permute-start.2 = (bf16[168,256]{1,0:T(8,128)(2,1)}, bf16[168,256]{1,0:T(8,128)(2,1)S(1)}, u32[]{:S(2)}, u32[]{:S(2)}) collective-permute-start(bf16[168,256]{1,0:T(8,128)(2,1)} %param.6), channel_id=1, source_target_pairs={{0,12},{4,16},{8,20},{12,24},{16,28},{20,32},{24,36},{28,40},{32,4... | collective-permute-start | bytes 258056 | tf_op jit(solution)/shard_map/ppermute | solution.py:10
  6.1 2.9 %collective-permute-start.3 = (bf16[168,256]{1,0:T(8,128)(2,1)}, bf16[168,256]{1,0:T(8,128)(2,1)S(1)}, u32[]{:S(2)}, u32[]{:S(2)}) collective-permute-start(bf16[168,256]{1,0:T(8,128)(2,1)} %param.6), channel_id=1, source_target_pairs={{0,16},{4,20},{8,24},{12,28},{16,32},{20,36},{24,40},{28,44},{32,4... | collective-permute-start | bytes 258056 | tf_op jit(solution)/shard_map/ppermute | solution.py:10
  9.0 2.9 %collective-permute-start.4 = (bf16[168,256]{1,0:T(8,128)(2,1)}, bf16[168,256]{1,0:T(8,128)(2,1)S(1)}, u32[]{:S(2)}, u32[]{:S(2)}) collective-permute-start(bf16[168,256]{1,0:T(8,128)(2,1)} %param.6), channel_id=1, source_target_pairs={{0,20},{4,24},{8,28},{12,32},{16,36},{20,40},{24,44},{28,48},{32,5... | collective-permute-start | bytes 258056 | tf_op jit(solution)/shard_map/ppermute | solution.py:10
  13.6 0.9 fusion.9
  15.4 0.9 fusion.7
  17.1 6.9 %dynamic-slice_bitcast_fusion = bf16[672,168,12]{1,0,2:T(8,128)(2,1)} fusion(bf16[12,672,672]{2,1,0:T(8,128)(2,1)} %param.7, s32[]{:T(128)S(6)} %select_n.100), kind=kLoop, calls=%fused_computation | loop fusion | bytes 5419012 | tf_op jit(solution)/shard_map/transpose | solution.py:50
  24.0 7.2 %copy.7 = bf16[672,168,12]{0,2,1:T(8,128)(2,1)} copy(bf16[672,168,12]{1,0,2:T(8,128)(2,1)} %dynamic-slice_bitcast_fusion) | data formatting | bytes 5419008 | tf_op jit(solution)/shard_map/transpose | solution.py:50
  31.2 6.6 %reshape.1312 = bf16[672,2016]{0,1:T(8,128)(2,1)} reshape(bf16[672,168,12]{0,2,1:T(8,128)(2,1)} %copy.7) | data formatting | bytes 5419008 | tf_op jit(solution)/shard_map/reshape | solution.py:50
  38.3 3.7 %add_convert_fusion.5 = bf16[256,3072]{0,1:T(8,128)(2,1)S(1)} fusion(f32[3072]{0:T(1024)S(1)} %broadcast_in_dim.421, f32[3072]{0:T(1024)S(1)} %broadcast_in_dim.416, f32[3072]{0:T(1024)S(1)} %broadcast_in_dim.411, f32[3072]{0:T(1024)S(1)} %broadcast_in_dim.405, pred[3072]{0:T(1024)(128)(4,1)S(1)} %eq.1067, pred[3072]{0:T(1024)(128)(4,1)S(1)} %eq.1058, ...), kind=kLoop, calls=%fused_computation.18 | loop fusion | flops 9437184 | bytes 1896448 | tf_op jit(solution)/shard_map/convert_element_type | solution.py:34
  42.6 1.2 %reshape_reshape.18 = bf16[2016,256]{1,0:T(8,128)(2,1)S(1)} reshape(bf16[168,3072]{1,0:T(8,128)(2,1)S(1)} %fusion) | data formatting | bytes 2064384 | tf_op jit(solution)/shard_map/reshape;reshape | solution.py:64
  44.1 3.9 %fusion.11 = f32[672,256]{1,0:T(8,128)} fusion(bf16[672,2016]{0,1:T(8,128)(2,1)} %reshape.1312, bf16[2016,256]{1,0:T(8,128)(2,1)S(1)} %reshape_reshape.18), kind=kOutput, calls=%fused_computation.127 | convolution fusion | flops 693633024 | bytes 4429824 | tf_op jit(solution)/shard_map/dot_general | solution.py:65
  50.3 3.7 %add_convert_fusion.4 = bf16[256,3072]{0,1:T(8,128)(2,1)S(1)} fusion(f32[3072]{0:T(1024)S(1)} %broadcast_in_dim.441, f32[3072]{0:T(1024)S(1)} %broadcast_in_dim.436, f32[3072]{0:T(1024)S(1)} %broadcast_in_dim.431, f32[3072]{0:T(1024)S(1)} %broadcast_in_dim.426, pred[3072]{0:T(1024)(128)(4,1)S(1)} %eq.1103, pred[3072]{0:T(1024)(128)(4,1)S(1)} %eq.1094, ...), kind=kLoop, calls=%fused_computation.17 | loop fusion | flops 9437184 | bytes 1896448 | tf_op jit(solution)/shard_map/convert_element_type | solution.py:34
  54.0 3.7 %add_convert_fusion.3 = bf16[256,3072]{0,1:T(8,128)(2,1)S(1)} fusion(f32[3072]{0:T(1024)S(1)} %broadcast_in_dim.461, f32[3072]{0:T(1024)S(1)} %broadcast_in_dim.456, f32[3072]{0:T(1024)S(1)} %broadcast_in_dim.451, f32[3072]{0:T(1024)S(1)} %broadcast_in_dim.446, pred[3072]{0:T(1024)(128)(4,1)S(1)} %eq.1139, pred[3072]{0:T(1024)(128)(4,1)S(1)} %eq.1130, ...), kind=kLoop, calls=%fused_computation.16 | loop fusion | flops 9437184 | bytes 1896448 | tf_op jit(solution)/shard_map/convert_element_type | solution.py:34
  57.6 3.7 %add_convert_fusion.2 = bf16[256,3072]{0,1:T(8,128)(2,1)S(1)} fusion(f32[3072]{0:T(1024)S(1)} %broadcast_in_dim.481, f32[3072]{0:T(1024)S(1)} %broadcast_in_dim.476, f32[3072]{0:T(1024)S(1)} %broadcast_in_dim.471, f32[3072]{0:T(1024)S(1)} %broadcast_in_dim.466, pred[3072]{0:T(1024)(128)(4,1)S(1)} %eq.1175, pred[3072]{0:T(1024)(128)(4,1)S(1)} %eq.1166, ...), kind=kLoop, calls=%fused_computation.15 | loop fusion | flops 9437184 | bytes 1896448 | tf_op jit(solution)/shard_map/convert_element_type | solution.py:34
  61.3 3.7 %add_convert_fusion.1 = bf16[256,3072]{0,1:T(8,128)(2,1)S(1)} fusion(f32[3072]{0:T(1024)S(1)} %broadcast_in_dim.501, f32[3072]{0:T(1024)S(1)} %broadcast_in_dim.496, f32[3072]{0:T(1024)S(1)} %broadcast_in_dim.491, f32[3072]{0:T(1024)S(1)} %broadcast_in_dim.486, pred[3072]{0:T(1024)(128)(4,1)S(1)} %eq.1211, pred[3072]{0:T(1024)(128)(4,1)S(1)} %eq.1202, ...), kind=kLoop, calls=%fused_computation.14 | loop fusion | flops 9437184 | bytes 1896448 | tf_op jit(solution)/shard_map/convert_element_type | solution.py:34
  65.0 3.9 %add_convert_fusion = bf16[256,3072]{0,1:T(8,128)(2,1)S(1)} fusion(f32[3072]{0:T(1024)S(1)} %broadcast_in_dim.521, f32[3072]{0:T(1024)S(1)} %broadcast_in_dim.516, f32[3072]{0:T(1024)S(1)} %broadcast_in_dim.511, f32[3072]{0:T(1024)S(1)} %broadcast_in_dim.506, pred[3072]{0:T(1024)(128)(4,1)S(1)} %eq.1247, pred[3072]{0:T(1024)(128)(4,1)S(1)} %eq.1238, ...), kind=kLoop, calls=%fused_computation.13 | loop fusion | flops 9437184 | bytes 1896448 | tf_op jit(solution)/shard_map/convert_element_type | solution.py:34
  69.6 1.7 %fusion.2 = bf16[168,3072]{1,0:T(8,128)(2,1)} fusion(bf16[256,3072]{0,1:T(8,128)(2,1)S(1)} %add_convert_fusion.3, bf16[168,256]{1,0:T(8,128)(2,1)S(1)} %collective-permute-done.1), kind=kOutput, calls=%fused_computation.9 | convolution fusion | flops 264757248 | bytes 2691072 | tf_op jit(solution)/shard_map/dot_general | solution.py:38
  71.2 1.6 %fusion.3 = bf16[168,3072]{1,0:T(8,128)(2,1)} fusion(bf16[256,3072]{0,1:T(8,128)(2,1)S(1)} %add_convert_fusion.2, bf16[168,256]{1,0:T(8,128)(2,1)S(1)} %collective-permute-done.2), kind=kOutput, calls=%fused_computation.10 | convolution fusion | flops 264757248 | bytes 2691072 | tf_op jit(solution)/shard_map/dot_general | solution.py:38
  72.9 1.7 %fusion.4 = bf16[168,3072]{1,0:T(8,128)(2,1)} fusion(bf16[256,3072]{0,1:T(8,128)(2,1)S(1)} %add_convert_fusion.1, bf16[168,256]{1,0:T(8,128)(2,1)S(1)} %collective-permute-done.3), kind=kOutput, calls=%fused_computation.11 | convolution fusion | flops 264757248 | bytes 2691072 | tf_op jit(solution)/shard_map/dot_general | solution.py:38
  74.6 2.1 %reshape_reshape.19 = bf16[2016,256]{1,0:T(8,128)(2,1)} reshape(bf16[168,3072]{1,0:T(8,128)(2,1)S(1)} %fusion.1) | data formatting | bytes 2064384 | tf_op jit(solution)/shard_map/reshape;reshape | solution.py:64
  76.7 3.2 %reshape_reshape.20 = bf16[2016,256]{1,0:T(8,128)(2,1)} reshape(bf16[168,3072]{1,0:T(8,128)(2,1)} %fusion.2) | data formatting | bytes 2064384 | tf_op jit(solution)/shard_map/reshape;reshape | solution.py:64
  80.0 3.1 %reshape_reshape.21 = bf16[2016,256]{1,0:T(8,128)(2,1)} reshape(bf16[168,3072]{1,0:T(8,128)(2,1)} %fusion.3) | data formatting | bytes 2064384 | tf_op jit(solution)/shard_map/reshape;reshape | solution.py:64
  83.1 2.2 %reshape_reshape.22 = bf16[2016,256]{1,0:T(8,128)(2,1)} reshape(bf16[168,3072]{1,0:T(8,128)(2,1)S(1)} %copy-done) | data formatting | bytes 2064384 | tf_op jit(solution)/shard_map/reshape;reshape | solution.py:64
  85.9 1.2 %reshape_reshape.23 = bf16[2016,256]{1,0:T(8,128)(2,1)S(1)} reshape(bf16[168,3072]{1,0:T(8,128)(2,1)S(1)} %fusion.5) | data formatting | bytes 2064384 | tf_op jit(solution)/shard_map/reshape;reshape | solution.py:64
  87.2 3.3 %convolution_add_fusion.4 = f32[672,256]{1,0:T(8,128)S(1)} fusion(f32[672,256]{1,0:T(8,128)S(1)} %copy-done.7, bf16[672,2016]{0,1:T(8,128)(2,1)} %reshape.1312, bf16[2016,256]{1,0:T(8,128)(2,1)} %reshape_reshape.19), kind=kOutput, calls=%fused_computation.47 | convolution fusion | flops 693805056 | bytes 5117952 | tf_op jit(solution)/shard_map/dot_general | solution.py:65
  90.6 1.0 convolution_add_fusion.3
  91.8 1.0 convolution_add_fusion.2
  93.0 1.0 convolution_add_fusion.1
  94.1 1.1 %fusion.6 = bf16[672,256]{1,0:T(8,128)(2,1)S(1)} fusion(f32[672,256]{1,0:T(8,128)S(1)} %convolution_add_fusion.1, bf16[672,2016]{0,1:T(8,128)(2,1)S(1)} %copy-done.1, bf16[2016,256]{1,0:T(8,128)(2,1)S(1)} %reshape_reshape.23), kind=kOutput, calls=%fused_computation.48 | convolution fusion | flops 693977088 | bytes 4773888 | tf_op jit(solution)/shard_map/dot_general | solution.py:65
  95.2 10.8 %all_to_all.5 = bf16[4,168,256]{2,1,0:T(8,128)(2,1)S(1)} all-to-all(bf16[4,168,256]{2,1,0:T(8,128)(2,1)S(1)} %bitcast.209), channel_id=1, replica_groups=mesh['blk'=64,'deg'=4] {'deg'}, dimensions={0} | all-to-all | bytes 688128 | tf_op jit(solution)/shard_map/all_to_all | solution.py:21
  (138 shorter events, 8.8 us)
Async XLA Ops:
  0.0 68.9 %collective-permute-start = (bf16[168,256]{1,0:T(8,128)(2,1)}, bf16[168,256]{1,0:T(8,128)(2,1)S(1)}, u32[]{:S(2)}, u32[]{:S(2)}) collective-permute-start(bf16[168,256]{1,0:T(8,128)(2,1)} %param.6), channel_id=1, source_target_pairs={{0,4},{4,8},{8,12},{12,16},{16,20},{20,24},{24,28},{28,32},{32,36}... | collective-permute-start | bytes 258056 | tf_op jit(solution)/shard_map/ppermute | solution.py:10
  0.9 68.6 %collective-permute-start.1 = (bf16[168,256]{1,0:T(8,128)(2,1)}, bf16[168,256]{1,0:T(8,128)(2,1)S(1)}, u32[]{:S(2)}, u32[]{:S(2)}) collective-permute-start(bf16[168,256]{1,0:T(8,128)(2,1)} %param.6), channel_id=1, source_target_pairs={{0,8},{4,12},{8,16},{12,20},{16,24},{20,28},{24,32},{28,36},{32,40... | collective-permute-start | bytes 258056 | tf_op jit(solution)/shard_map/ppermute | solution.py:10
  4.1 67.2 %collective-permute-start.2 = (bf16[168,256]{1,0:T(8,128)(2,1)}, bf16[168,256]{1,0:T(8,128)(2,1)S(1)}, u32[]{:S(2)}, u32[]{:S(2)}) collective-permute-start(bf16[168,256]{1,0:T(8,128)(2,1)} %param.6), channel_id=1, source_target_pairs={{0,12},{4,16},{8,20},{12,24},{16,28},{20,32},{24,36},{28,40},{32,4... | collective-permute-start | bytes 258056 | tf_op jit(solution)/shard_map/ppermute | solution.py:10
  6.1 66.8 %collective-permute-start.3 = (bf16[168,256]{1,0:T(8,128)(2,1)}, bf16[168,256]{1,0:T(8,128)(2,1)S(1)}, u32[]{:S(2)}, u32[]{:S(2)}) collective-permute-start(bf16[168,256]{1,0:T(8,128)(2,1)} %param.6), channel_id=1, source_target_pairs={{0,16},{4,20},{8,24},{12,28},{16,32},{20,36},{24,40},{28,44},{32,4... | collective-permute-start | bytes 258056 | tf_op jit(solution)/shard_map/ppermute | solution.py:10
  9.0 76.3 %collective-permute-start.4 = (bf16[168,256]{1,0:T(8,128)(2,1)}, bf16[168,256]{1,0:T(8,128)(2,1)S(1)}, u32[]{:S(2)}, u32[]{:S(2)}) collective-permute-start(bf16[168,256]{1,0:T(8,128)(2,1)} %param.6), channel_id=1, source_target_pairs={{0,20},{4,24},{8,28},{12,32},{16,36},{20,40},{24,44},{28,48},{32,5... | collective-permute-start | bytes 258056 | tf_op jit(solution)/shard_map/ppermute | solution.py:10
  31.1 10.8 %copy-start.5 = (bf16[168,256]{1,0:T(8,128)(2,1)S(1)}, bf16[168,256]{1,0:T(8,128)(2,1)}, u32[]{:S(2)}) copy-start(bf16[168,256]{1,0:T(8,128)(2,1)} %param.6) | copy-start | bytes 258052
  76.7 6.3 %copy-start = (bf16[168,3072]{1,0:T(8,128)(2,1)S(1)}, bf16[168,3072]{1,0:T(8,128)(2,1)}, u32[]{:S(2)}) copy-start(bf16[168,3072]{1,0:T(8,128)(2,1)} %fusion.4) | copy-start | bytes 3096580
  83.1 4.1 %copy-start.7 = (f32[672,256]{1,0:T(8,128)S(1)}, f32[672,256]{1,0:T(8,128)}, u32[]{:S(2)}) copy-start(f32[672,256]{1,0:T(8,128)} %fusion.11) | copy-start | bytes 2064388
  87.2 3.4 %copy-start.1 = (bf16[672,2016]{0,1:T(8,128)(2,1)S(1)}, bf16[672,2016]{0,1:T(8,128)(2,1)}, u32[]{:S(2)}) copy-start(bf16[672,2016]{0,1:T(8,128)(2,1)} %reshape.1312) | copy-start | bytes 8128516
  87.2 3.4 %copy-start.4 = (bf16[2016,256]{1,0:T(8,128)(2,1)S(1)}, bf16[2016,256]{1,0:T(8,128)(2,1)}, u32[]{:S(2)}) copy-start(bf16[2016,256]{1,0:T(8,128)(2,1)} %reshape_reshape.20) | copy-start | bytes 3096580
  90.6 1.2 %copy-start.3 = (bf16[2016,256]{1,0:T(8,128)(2,1)S(1)}, bf16[2016,256]{1,0:T(8,128)(2,1)}, u32[]{:S(2)}) copy-start(bf16[2016,256]{1,0:T(8,128)(2,1)} %reshape_reshape.21) | copy-start | bytes 3096580
  91.8 1.2 %copy-start.2 = (bf16[2016,256]{1,0:T(8,128)(2,1)S(1)}, bf16[2016,256]{1,0:T(8,128)(2,1)}, u32[]{:S(2)}) copy-start(bf16[2016,256]{1,0:T(8,128)(2,1)} %reshape_reshape.22) | copy-start | bytes 3096580
  94.0 11.9 %copy-start.6 = (f32[168,256]{1,0:T(8,128)S(1)}, f32[168,256]{1,0:T(8,128)}, u32[]{:S(2)}) copy-start(f32[168,256]{1,0:T(8,128)} %param.8) | copy-start | bytes 516100
where the time goes:
time: 108 us; the launch traced here: 107 us
  local copies, waits for them, and re-layouts  38 us (35%)
  other arithmetic  26.5 us (25%)
  matrix products  18.5 us (17%)
  starting transfers between devices  11.9 us (11%)
  blocking collectives  10.8 us (10%)
    convert_element_type x6, other arithmetic, selection(): table.astype(jnp.bfloat16).reshape(sphere_count, classes * indices.shape[1])  22.2 us
    transpose x2, local copies, waits for them, and re-layouts, local(): jnp.transpose(weight_cols, (1, 2, 0))  14.1 us
    another operation x6, local copies, waits for them, and re-layouts, local(): operand = combined.reshape(combined.shape[0] * classes, sphere_count)  13.1 us
    ppermute x5, starting transfers between devices, from_behind(): return lax.ppermute(value, axis, pairs)  11.9 us
    dot_general x6, matrix products, local(): jnp.dot(weight_flat, operand, preferred_element_type=jnp.float32)  11.4 us
    all_to_all x1, blocking collectives, summed_on_arrival(): tiles = lax.all_to_all(cut_along(x, dim, size), axis, 0, 0, tiled=True)  10.8 us
    dot_general x6, matrix products, combine(): mixed = jnp.dot(visiting, table, preferred_element_type=jnp.float32)  7.05 us
    reshape x1, local copies, waits for them, and re-layouts, local(): jnp.transpose(weight_cols, (1, 2, 0))  6.63 us
  transfers between devices with their start and end apart: 5, of which 0 were waited for; matrix products, arithmetic and copies ran while one was open for 68% of the time, Pallas kernels for 0%

commit v1 on v0

v1 whole, which is shorter than its diff:
```python
import functools

import jax
import jax.numpy as jnp
from jax import lax
from jax.experimental import pallas as pl
from jax.experimental.pallas import tpu as pltpu
from jax.sharding import PartitionSpec as P

VMEM = pl.BlockSpec(memory_space=pltpu.VMEM)


def prepare(position, operators, sources, kinds, scales, table, weights, stage, arrived):
    classes, full, _ = operators.shape
    visits, slots, spheres = sources.shape
    rows = weights.shape[2]
    deg = position[0]
    for c in range(classes):
        pltpu.make_async_copy(operators.at[c], stage.at[c], arrived.at[c]).start()

    sphere = lax.broadcasted_iota(jnp.int32, (spheres, spheres), 0).astype(jnp.float32).astype(jnp.bfloat16)

    def visit(s, _):
        picked = sources[s].astype(jnp.float32).astype(jnp.bfloat16)
        kind = kinds[s]
        scale = scales[s]
        zero = jnp.zeros((), jnp.bfloat16)
        hits = [
            jnp.where(sphere == picked[k : k + 1, :], scale[k : k + 1, :], zero) for k in range(slots)
        ]
        for c in range(classes):
            own = jnp.where(kind == c, 1.0, 0.0).astype(jnp.bfloat16)
            terms = [hits[k] * own[k : k + 1, :] for k in range(slots)]
            while len(terms) > 1:
                terms = [sum(terms[i + 1 : i + 2], terms[i]) for i in range(0, len(terms), 2)]
            table[c, s] = terms[0]
        return 0

    lax.fori_loop(0, visits, visit, 0)

    row = lax.broadcasted_iota(jnp.int32, (full, rows), 0)
    column = lax.broadcasted_iota(jnp.int32, (full, rows), 1)
    pick = jnp.where(row == column + deg * rows, 1.0, 0.0).astype(jnp.bfloat16)

    def operator(c, _):
        pltpu.make_async_copy(operators.at[c], stage.at[c], arrived.at[c]).wait()
        own = jnp.dot(stage[c], pick, preferred_element_type=jnp.float32)
        for d in range(full // rows):
            weights[c, jnp.bitwise_xor(deg, d)] = own[d * rows : (d + 1) * rows].astype(jnp.bfloat16)
        return 0

    lax.fori_loop(0, classes, operator, 0)


def interact(groups, *refs):
    visiting, table, weights = refs[:-6], refs[-6], refs[-5]
    outs = refs[-4:]
    classes = table.shape[0]
    combined = []
    for c in range(classes):
        mixed = jnp.dot(visiting[0][...], table[c, 0], preferred_element_type=jnp.float32)
        for s in range(1, len(visiting)):
            mixed += jnp.dot(visiting[s][...], table[c, s], preferred_element_type=jnp.float32)
        combined.append(mixed.astype(jnp.bfloat16))
    for d in range(groups - 1, -1, -1):
        field = jnp.dot(weights[0, d], combined[0], preferred_element_type=jnp.float32)
        for c in range(1, classes):
            field += jnp.dot(weights[c, d], combined[c], preferred_element_type=jnp.float32)
        outs[d][...] = field.astype(outs[d].dtype)


def local(source, operators, mie_factor, pair_source, pair_class, pair_scale):
    rows, spheres = source.shape
    classes, full, _ = operators.shape
    visits = pair_source.shape[0]
    groups = full // rows
    blocks = lax.axis_size("blk")
    visiting = [source]
    for s in range(1, visits):
        visiting.append(lax.ppermute(source, "blk", [(b, (b + s) % blocks) for b in range(blocks)]))

    position = jnp.asarray(lax.axis_index("deg"), jnp.int32).reshape(1)
    table, weights = pl.pallas_call(
        prepare,
        out_shape=(
            jax.ShapeDtypeStruct((classes, visits, spheres, spheres), jnp.bfloat16),
            jax.ShapeDtypeStruct((classes, groups, rows, rows), jnp.bfloat16),
        ),
        in_specs=[pl.BlockSpec(memory_space=pltpu.SMEM), pl.BlockSpec(memory_space=pltpu.HBM)] + [VMEM] * 3,
        out_specs=(VMEM, VMEM),
        scratch_shapes=[
            pltpu.VMEM((classes, full, full), jnp.bfloat16),
            pltpu.SemaphoreType.DMA((classes,)),
        ],
        compiler_params=pltpu.CompilerParams(vmem_limit_bytes=24 * 2**20),
        cost_estimate=pl.CostEstimate(
            flops=2 * classes * full * full * rows, bytes_accessed=2 * operators.size, transcendentals=0
        ),
        name="prepare",
    )(position, operators, pair_source, pair_class, pair_scale)

    outs = pl.pallas_call(
        functools.partial(interact, groups),
        out_shape=(jax.ShapeDtypeStruct((rows, spheres), jnp.float32),)
        + (jax.ShapeDtypeStruct((rows, spheres), jnp.bfloat16),) * (groups - 1),
        in_specs=[VMEM] * (visits + 2),
        out_specs=(VMEM,) * groups,
        compiler_params=pltpu.CompilerParams(vmem_limit_bytes=24 * 2**20),
        cost_estimate=pl.CostEstimate(
            flops=2 * rows * spheres * classes * (visits * spheres + full), bytes_accessed=2 * table.size, transcendentals=0
        ),
        name="interact",
    )(*visiting, table, weights)

    field = outs[0]
    for d in range(1, groups):
        other = lax.ppermute(outs[d], "deg", [(i, i ^ d) for i in range(groups)])
        field = field + other.astype(jnp.float32)
    return source.astype(jnp.float32) - mie_factor * field


def solution(mesh):
    return jax.shard_map(
        local,
        mesh=mesh,
        in_specs=(
            P("deg", "blk"),
            P(),
            P("deg", "blk"),
            P(None, None, "blk"),
            P(None, None, "blk"),
            P(None, None, "blk"),
        ),
        out_specs=P("deg", "blk"),
        check_vma=False,
    )
```

time: 108 us -> 45.2 us (0.42)
  local copies, waits for them, and re-layouts: 38 us -> 6.71 us
  other arithmetic: 26.5 us -> 0.74 us
  matrix products: 18.5 us -> 0 us
  Pallas kernels: 0 us -> 16 us
  blocking collectives: 10.8 us -> 0 us
  starting transfers between devices: 11.9 us -> 17 us
  waiting for transfers between devices: 0.01 us -> 4.39 us
    convert_element_type x6 -> x0, other arithmetic: 22.2 us -> none  [selection(): table.astype(jnp.bfloat16).reshape(sphere_count, classes * indices.shape[1])]
    dot_general x12 -> x0, matrix products: 18.5 us -> none  [the longest x6 11.4 us: local(): jnp.dot(weight_flat, operand, preferred_element_type=jnp.float32)]
    pallas_call x0 -> x2, Pallas kernels: none -> 16 us  [the longest x1 13 us: local(): pl.pallas_call(prepare, out_shape=(jax.ShapeDtypeStruct((classes, visits,...]
    transpose x2 -> x0, local copies, waits for them, and re-layouts: 14.1 us -> none  [local(): jnp.transpose(weight_cols, (1, 2, 0))]
    another operation x6 -> x0, local copies, waits for them, and re-layouts: 13.1 us -> none  [local(): operand = combined.reshape(combined.shape[0] * classes, sphere_count)]
    all_to_all x1 -> x0, blocking collectives: 10.8 us -> none  [summed_on_arrival(): tiles = lax.all_to_all(cut_along(x, dim, size), axis, 0, 0, tiled=True)]
    reshape x1 -> x0, local copies, waits for them, and re-layouts: 6.63 us -> none  [local(): jnp.transpose(weight_cols, (1, 2, 0))]
    unnamed x16 -> x12, local copies, waits for them, and re-layouts: 0.39 us -> 6.71 us
  transfers between devices with their start and end apart: 5 -> 8, of which waited for: 0 -> 2; matrix products, arithmetic and copies ran while one was open for 68% -> 0% of each run, Pallas kernels for 0% -> 29%
where the time goes in v1:
time: 45.2 us; the launch traced here: 45 us
  starting transfers between devices  17 us (38%)
  Pallas kernels  16 us (35%)
  local copies, waits for them, and re-layouts  6.71 us (15%)
  waiting for transfers between devices  4.39 us (10%)
  other arithmetic  0.74 us (2%)
    ppermute x5, starting transfers between devices, local(): lax.ppermute(source, 'blk', [(b, (b + s) % blocks) for b in range(blocks)])  13.1 us
    pallas_call x1, Pallas kernels, local(): pl.pallas_call(prepare, out_shape=(jax.ShapeDtypeStruct((classes, visits,...  13 us
    unnamed x12, local copies, waits for them, and re-layouts  6.71 us
    ppermute x3, waiting for transfers between devices, local(): other = lax.ppermute(outs[d], 'deg', [(i, i ^ d) for i in range(groups)])  4.38 us
    ppermute x3, starting transfers between devices, local(): other = lax.ppermute(outs[d], 'deg', [(i, i ^ d) for i in range(groups)])  3.89 us
    pallas_call x1, Pallas kernels, local(): pl.pallas_call(functools.partial(interact, groups), out_shape=(jax.ShapeD...  2.99 us
  transfers between devices with their start and end apart: 8, of which 2 were waited for; matrix products, arithmetic and copies ran while one was open for 0% of the time, Pallas kernels for 29%

profile of v1, /device:TPU:69, one launch (start us, length us, event | category | flops | bytes accessed | tf_op | source)
XLA Modules:
  0.0 45.0 jit_solution(14591921080336048530)
XLA Ops:
  0.0 2.9 %collective-permute-start.3 = (bf16[168,256]{1,0:T(8,128)(2,1)}, bf16[168,256]{1,0:T(8,128)(2,1)S(1)}, u32[]{:S(2)}, u32[]{:S(2)}) collective-permute-start(bf16[168,256]{1,0:T(8,128)(2,1)} %refs_0_.1), channel_id=1, source_target_pairs={{0,16},{4,20},{8,24},{12,28},{16,32},{20,36},{24,40},{28,44},{32,4... | collective-permute-start | bytes 258056 | tf_op jit(solution)/shard_map/ppermute | solution.py:80
  2.9 1.4 %collective-permute-start.2 = (bf16[168,256]{1,0:T(8,128)(2,1)}, bf16[168,256]{1,0:T(8,128)(2,1)S(1)}, u32[]{:S(2)}, u32[]{:S(2)}) collective-permute-start(bf16[168,256]{1,0:T(8,128)(2,1)} %refs_0_.1), channel_id=1, source_target_pairs={{0,12},{4,16},{8,20},{12,24},{16,28},{20,32},{24,36},{28,40},{32,4... | collective-permute-start | bytes 258056 | tf_op jit(solution)/shard_map/ppermute | solution.py:80
  4.3 2.5 %collective-permute-start.1 = (bf16[168,256]{1,0:T(8,128)(2,1)}, bf16[168,256]{1,0:T(8,128)(2,1)S(1)}, u32[]{:S(2)}, u32[]{:S(2)}) collective-permute-start(bf16[168,256]{1,0:T(8,128)(2,1)} %refs_0_.1), channel_id=1, source_target_pairs={{0,8},{4,12},{8,16},{12,20},{16,24},{20,28},{24,32},{28,36},{32,40... | collective-permute-start | bytes 258056 | tf_op jit(solution)/shard_map/ppermute | solution.py:80
  6.7 2.2 %collective-permute-start = (bf16[168,256]{1,0:T(8,128)(2,1)}, bf16[168,256]{1,0:T(8,128)(2,1)S(1)}, u32[]{:S(2)}, u32[]{:S(2)}) collective-permute-start(bf16[168,256]{1,0:T(8,128)(2,1)} %refs_0_.1), channel_id=1, source_target_pairs={{0,4},{4,8},{8,12},{12,16},{16,20},{20,24},{24,28},{28,32},{32,36}... | collective-permute-start | bytes 258056 | tf_op jit(solution)/shard_map/ppermute | solution.py:80
  9.0 4.2 %collective-permute-start.4 = (bf16[168,256]{1,0:T(8,128)(2,1)}, bf16[168,256]{1,0:T(8,128)(2,1)S(1)}, u32[]{:S(2)}, u32[]{:S(2)}) collective-permute-start(bf16[168,256]{1,0:T(8,128)(2,1)} %refs_0_.1), channel_id=1, source_target_pairs={{0,20},{4,24},{8,28},{12,32},{16,36},{20,40},{24,44},{28,48},{32,5... | collective-permute-start | bytes 258056 | tf_op jit(solution)/shard_map/ppermute | solution.py:80
  13.1 0.0 copy-start
  13.1 4.5 %copy-done = bf16[12,672,672]{2,1,0:T(8,128)(2,1)S(1)} copy-done((bf16[12,672,672]{2,1,0:T(8,128)(2,1)S(1)}, bf16[12,672,672]{2,1,0:T(8,128)(2,1)}, u32[]{:S(2)}) %copy-start) | copy-done | bytes 10838040
  17.6 0.0 copy-start.2
  17.6 0.7 %copy-done.2 = s32[6,4,256]{2,1,0:T(4,128)S(1)} copy-done((s32[6,4,256]{2,1,0:T(4,128)S(1)}, s32[6,4,256]{2,1,0:T(4,128)}, u32[]{:S(2)}) %copy-start.2) | copy-done | bytes 24600
  18.4 0.0 copy-start.3
  18.4 0.7 %copy-done.3 = s32[6,4,256]{2,1,0:T(4,128)S(1)} copy-done((s32[6,4,256]{2,1,0:T(4,128)S(1)}, s32[6,4,256]{2,1,0:T(4,128)}, u32[]{:S(2)}) %copy-start.3) | copy-done | bytes 24600
  19.1 0.0 copy-start.4
  19.1 0.7 %copy-done.4 = bf16[6,4,256]{2,1,0:T(4,128)(2,1)S(1)} copy-done((bf16[6,4,256]{2,1,0:T(4,128)(2,1)S(1)}, bf16[6,4,256]{2,1,0:T(4,128)(2,1)}, u32[]{:S(2)}) %copy-start.4) | copy-done | bytes 12312
  19.8 0.0 copy-start.1
  19.8 13.0 %prepare.1 = (bf16[12,6,256,256]{3,2,1,0:T(8,128)(2,1)S(1)}, bf16[12,4,168,168]{3,2,1,0:T(8,128)(2,1)S(1)}) custom-call(s32[1]{0:T(128)} %bitcast.position, bf16[12,672,672]{2,1,0:T(8,128)(2,1)S(1)} %copy-done, s32[6,4,256]{2,1,0:T(4,128)S(1)} %copy-done.2, s32[6,4,256]{2,1,0:T(4,128)S(1)} %copy-done.3, bf16[6,4,256]{2,1,0:T(4,128)(2,1)S(1)} %copy-done.4), custom_call_target="tpu_custom_call" | custom-call | flops 1820786688 | bytes 10838016 | tf_op jit(solution)/shard_map/prepare/pallas_call | solution.py:83
  32.9 0.0 copy-start.5
  32.9 0.0 collective-permute-done.3.refs_4_
  32.9 0.0 collective-permute-done.2.refs_3_
  32.9 0.0 collective-permute-done.1.refs_2_
  32.9 0.0 collective-permute-done.refs_1_
  32.9 0.0 collective-permute-done.4.refs_5_
  32.9 0.0 copy-done.1
  32.9 3.0 %interact.1 = (f32[168,256]{1,0:T(8,128)S(1)}, bf16[168,256]{1,0:T(8,128)(2,1)S(1)}, bf16[168,256]{1,0:T(8,128)(2,1)S(1)}, bf16[168,256]{1,0:T(8,128)(2,1)S(1)}) custom-call(bf16[168,256]{1,0:T(8,128)(2,1)S(1)} %copy-done.1, bf16[168,256]{1,0:T(8,128)(2,1)S(1)} %collective-permute-done.refs_1_, bf16[168,256]{1,0:T(8,128)(2,1)S(1)} %collective-permute-done.1.refs_2_, ...), custom_call_target="tpu_custom_call" | custom-call | flops 2279079936 | bytes 9437184 | tf_op jit(solution)/shard_map/interact/pallas_call | solution.py:102
  35.9 2.2 %collective-permute-start.5 = (bf16[168,256]{1,0:T(8,128)(2,1)S(1)}, bf16[168,256]{1,0:T(8,128)(2,1)S(1)}, u32[]{:S(2)}, u32[]{:S(2)}) collective-permute-start(bf16[168,256]{1,0:T(8,128)(2,1)S(1)} %get-tuple-element.14), channel_id=1, source_target_pairs={{0,1},{1,0},{2,3},{3,2},{4,5},{5,4},{6,7},{7,6},{8,9},{9,8},{10,11... | collective-permute-start | bytes 258056 | tf_op jit(solution)/shard_map/ppermute | solution.py:117
  38.1 1.3 %collective-permute-start.6 = (bf16[168,256]{1,0:T(8,128)(2,1)S(1)}, bf16[168,256]{1,0:T(8,128)(2,1)S(1)}, u32[]{:S(2)}, u32[]{:S(2)}) collective-permute-start(bf16[168,256]{1,0:T(8,128)(2,1)S(1)} %get-tuple-element.15), channel_id=1, source_target_pairs={{0,2},{1,3},{2,0},{3,1},{4,6},{5,7},{6,4},{7,5},{8,10},{9,11},{10,... | collective-permute-start | bytes 258056 | tf_op jit(solution)/shard_map/ppermute | solution.py:117
  39.4 0.4 collective-permute-start.7
  39.8 0.0 collective-permute-done.5
  39.8 2.3 %collective-permute-done.6 = bf16[168,256]{1,0:T(8,128)(2,1)S(1)} collective-permute-done((bf16[168,256]{1,0:T(8,128)(2,1)S(1)}, bf16[168,256]{1,0:T(8,128)(2,1)S(1)}, u32[]{:S(2)}, u32[]{:S(2)}) %collective-permute-start.6) | collective-permute-done | bytes 86048 | tf_op jit(solution)/shard_map/ppermute | solution.py:117
  42.1 2.1 %collective-permute-done.7 = bf16[168,256]{1,0:T(8,128)(2,1)S(1)} collective-permute-done((bf16[168,256]{1,0:T(8,128)(2,1)S(1)}, bf16[168,256]{1,0:T(8,128)(2,1)S(1)}, u32[]{:S(2)}, u32[]{:S(2)}) %collective-permute-start.7) | collective-permute-done | bytes 86048 | tf_op jit(solution)/shard_map/ppermute | solution.py:117
  44.2 0.0 copy-done.5
  44.2 0.7 %multiply_subtract_fusion = f32[168,256]{1,0:T(8,128)} fusion(f32[168,256]{1,0:T(8,128)S(1)} %copy-done.5, bf16[168,256]{1,0:T(8,128)(2,1)S(1)} %collective-permute-done.7, bf16[168,256]{1,0:T(8,128)(2,1)S(1)} %collective-permute-done.6, f32[168,256]{1,0:T(8,128)S(1)} %get-tuple-element.13, bf16[168,256]{1,0:T(8,128)(2,1)S(1)} %collective-permute-done.5, ...), kind=kLoop, calls=%fused_computation | loop fusion | flops 387072 | bytes 860160 | tf_op jit(solution)/shard_map/sub | solution.py:119
Async XLA Ops:
  0.0 32.9 %collective-permute-start.3 = (bf16[168,256]{1,0:T(8,128)(2,1)}, bf16[168,256]{1,0:T(8,128)(2,1)S(1)}, u32[]{:S(2)}, u32[]{:S(2)}) collective-permute-start(bf16[168,256]{1,0:T(8,128)(2,1)} %refs_0_.1), channel_id=1, source_target_pairs={{0,16},{4,20},{8,24},{12,28},{16,32},{20,36},{24,40},{28,44},{32,4... | collective-permute-start | bytes 258056 | tf_op jit(solution)/shard_map/ppermute | solution.py:80
  2.9 30.0 %collective-permute-start.2 = (bf16[168,256]{1,0:T(8,128)(2,1)}, bf16[168,256]{1,0:T(8,128)(2,1)S(1)}, u32[]{:S(2)}, u32[]{:S(2)}) collective-permute-start(bf16[168,256]{1,0:T(8,128)(2,1)} %refs_0_.1), channel_id=1, source_target_pairs={{0,12},{4,16},{8,20},{12,24},{16,28},{20,32},{24,36},{28,40},{32,4... | collective-permute-start | bytes 258056 | tf_op jit(solution)/shard_map/ppermute | solution.py:80
  4.3 28.6 %collective-permute-start.1 = (bf16[168,256]{1,0:T(8,128)(2,1)}, bf16[168,256]{1,0:T(8,128)(2,1)S(1)}, u32[]{:S(2)}, u32[]{:S(2)}) collective-permute-start(bf16[168,256]{1,0:T(8,128)(2,1)} %refs_0_.1), channel_id=1, source_target_pairs={{0,8},{4,12},{8,16},{12,20},{16,24},{20,28},{24,32},{28,36},{32,40... | collective-permute-start | bytes 258056 | tf_op jit(solution)/shard_map/ppermute | solution.py:80
  6.7 26.2 %collective-permute-start = (bf16[168,256]{1,0:T(8,128)(2,1)}, bf16[168,256]{1,0:T(8,128)(2,1)S(1)}, u32[]{:S(2)}, u32[]{:S(2)}) collective-permute-start(bf16[168,256]{1,0:T(8,128)(2,1)} %refs_0_.1), channel_id=1, source_target_pairs={{0,4},{4,8},{8,12},{12,16},{16,20},{20,24},{24,28},{28,32},{32,36}... | collective-permute-start | bytes 258056 | tf_op jit(solution)/shard_map/ppermute | solution.py:80
  9.0 23.9 %collective-permute-start.4 = (bf16[168,256]{1,0:T(8,128)(2,1)}, bf16[168,256]{1,0:T(8,128)(2,1)S(1)}, u32[]{:S(2)}, u32[]{:S(2)}) collective-permute-start(bf16[168,256]{1,0:T(8,128)(2,1)} %refs_0_.1), channel_id=1, source_target_pairs={{0,20},{4,24},{8,28},{12,32},{16,36},{20,40},{24,44},{28,48},{32,5... | collective-permute-start | bytes 258056 | tf_op jit(solution)/shard_map/ppermute | solution.py:80
  13.1 4.5 %copy-start = (bf16[12,672,672]{2,1,0:T(8,128)(2,1)S(1)}, bf16[12,672,672]{2,1,0:T(8,128)(2,1)}, u32[]{:S(2)}) copy-start(bf16[12,672,672]{2,1,0:T(8,128)(2,1)} %operators.1) | copy-start | bytes 32514052
  17.6 0.7 %copy-start.2 = (s32[6,4,256]{2,1,0:T(4,128)S(1)}, s32[6,4,256]{2,1,0:T(4,128)}, u32[]{:S(2)}) copy-start(s32[6,4,256]{2,1,0:T(4,128)} %sources.1) | copy-start | bytes 73732
  18.4 0.7 %copy-start.3 = (s32[6,4,256]{2,1,0:T(4,128)S(1)}, s32[6,4,256]{2,1,0:T(4,128)}, u32[]{:S(2)}) copy-start(s32[6,4,256]{2,1,0:T(4,128)} %kinds.1) | copy-start | bytes 73732
  19.1 0.7 %copy-start.4 = (bf16[6,4,256]{2,1,0:T(4,128)(2,1)S(1)}, bf16[6,4,256]{2,1,0:T(4,128)(2,1)}, u32[]{:S(2)}) copy-start(bf16[6,4,256]{2,1,0:T(4,128)(2,1)} %scales.1) | copy-start | bytes 36868
  19.8 13.1 %copy-start.1 = (bf16[168,256]{1,0:T(8,128)(2,1)S(1)}, bf16[168,256]{1,0:T(8,128)(2,1)}, u32[]{:S(2)}) copy-start(bf16[168,256]{1,0:T(8,128)(2,1)} %refs_0_.1) | copy-start | bytes 258052
  32.9 11.3 %copy-start.5 = (f32[168,256]{1,0:T(8,128)S(1)}, f32[168,256]{1,0:T(8,128)}, u32[]{:S(2)}) copy-start(f32[168,256]{1,0:T(8,128)} %param.8) | copy-start | bytes 516100
  35.9 3.9 %collective-permute-start.5 = (bf16[168,256]{1,0:T(8,128)(2,1)S(1)}, bf16[168,256]{1,0:T(8,128)(2,1)S(1)}, u32[]{:S(2)}, u32[]{:S(2)}) collective-permute-start(bf16[168,256]{1,0:T(8,128)(2,1)S(1)} %get-tuple-element.14), channel_id=1, source_target_pairs={{0,1},{1,0},{2,3},{3,2},{4,5},{5,4},{6,7},{7,6},{8,9},{9,8},{10,11... | collective-permute-start | bytes 258056 | tf_op jit(solution)/shard_map/ppermute | solution.py:117
  38.1 4.0 %collective-permute-start.6 = (bf16[168,256]{1,0:T(8,128)(2,1)S(1)}, bf16[168,256]{1,0:T(8,128)(2,1)S(1)}, u32[]{:S(2)}, u32[]{:S(2)}) collective-permute-start(bf16[168,256]{1,0:T(8,128)(2,1)S(1)} %get-tuple-element.15), channel_id=1, source_target_pairs={{0,2},{1,3},{2,0},{3,1},{4,6},{5,7},{6,4},{7,5},{8,10},{9,11},{10,... | collective-permute-start | bytes 258056 | tf_op jit(solution)/shard_map/ppermute | solution.py:117
  39.4 4.8 %collective-permute-start.7 = (bf16[168,256]{1,0:T(8,128)(2,1)S(1)}, bf16[168,256]{1,0:T(8,128)(2,1)S(1)}, u32[]{:S(2)}, u32[]{:S(2)}) collective-permute-start(bf16[168,256]{1,0:T(8,128)(2,1)S(1)} %get-tuple-element.16), channel_id=1, source_target_pairs={{0,3},{1,2},{2,1},{3,0},{4,7},{5,6},{6,5},{7,4},{8,11},{9,10},{10,... | collective-permute-start | bytes 258056 | tf_op jit(solution)/shard_map/ppermute | solution.py:117

commit v2 on v1

v2 whole, which is shorter than its diff:
```python
import functools

import jax
import jax.numpy as jnp
from jax import lax
from jax.experimental import pallas as pl
from jax.experimental.pallas import tpu as pltpu
from jax.sharding import PartitionSpec as P


LANES = 128
STRIP = 32
EARLY = 4
SPHERE_BITS = 8
SCALE_BITS = 10
SCALE_UNIT = 512
VMEM = pl.BlockSpec(memory_space=pltpu.VMEM)


def prepare(codes, operators, table, weights, stage, arrived):
    classes, full, _ = operators.shape
    visits, slots, spheres = codes.shape
    rows = weights.shape[2]
    deg = lax.axis_index("deg")
    first = [d * rows // LANES * LANES for d in range(full // rows)]
    width = [min(-(-((d + 1) * rows - first[d]) // LANES) * LANES, full - first[d]) for d in range(full // rows)]

    def window(d, c):
        source, target = operators.at[c], stage.at[c]
        if width[d] % LANES == 0:
            source, target = (ref.at[:, first[d] : first[d] + width[d]] for ref in (source, target))
        return pltpu.make_async_copy(source, target, arrived.at[c])

    def each_group(body):
        for d in range(full // rows):
            pl.when(deg == d)(functools.partial(body, d))

    def fetch(d):
        for c in range(classes):
            window(d, c).start()

    each_group(fetch)

    def spread(x, k):
        return jnp.broadcast_to(x[k : k + 1, :], (STRIP, spheres))

    zero = jnp.zeros((), jnp.bfloat16)
    sphere = lax.broadcasted_iota(jnp.int32, (STRIP, spheres), 0).astype(jnp.float32).astype(jnp.bfloat16)

    def tables(s, before, after):
        kind = jnp.right_shift(codes[s], SPHERE_BITS + SCALE_BITS)
        picked = jnp.bitwise_and(jnp.right_shift(codes[s], SCALE_BITS), 2**SPHERE_BITS - 1)
        scale = jnp.bitwise_and(codes[s], 2**SCALE_BITS - 1).astype(jnp.float32) * (1.0 / SCALE_UNIT)
        picked, scale = picked.astype(jnp.float32).astype(jnp.bfloat16), scale.astype(jnp.bfloat16)
        picked = [spread(picked, k) for k in range(slots)]
        scale = [spread(scale, k) for k in range(slots)]
        mine = []
        for c in range(classes):
            flags = jnp.where(kind == c, 1.0, 0.0).astype(jnp.bfloat16)
            mine.append([spread(flags, k) for k in range(slots)])
        for turn, start in enumerate(range(0, spheres, STRIP)):
            work = before(turn)
            here = sphere + jnp.asarray(start, jnp.bfloat16)
            hits = [jnp.where(here == picked[k], scale[k], zero) for k in range(slots)]
            for c in range(classes):
                terms = [hits[k] * mine[c][k] for k in range(slots)]
                while len(terms) > 1:
                    terms = [sum(terms[i + 1 : i + 2], terms[i]) for i in range(0, len(terms), 2)]
                table[c, s, start : start + STRIP] = terms[0]
            after(work)

    def with_operators(d):
        row = lax.broadcasted_iota(jnp.int32, (width[d], rows), 0)
        column = lax.broadcasted_iota(jnp.int32, (width[d], rows), 1)
        pick = jnp.where(row == column + (d * rows - first[d]), 1.0, 0.0).astype(jnp.bfloat16)
        groups, turns = full // rows, spheres // STRIP
        share = classes // (visits - 2)

        def visit(s, _):
            base = (s - 1) * share
            for c in range(share):
                window(d, base + c).wait()

            def before(turn):
                done = []
                for chunk in range(turn * share * groups // turns, (turn + 1) * share * groups // turns):
                    c, g = base + chunk // groups, chunk % groups
                    part = stage[c, g * rows : (g + 1) * rows, first[d] : first[d] + width[d]]
                    done.append((c, g ^ d, jnp.dot(part, pick, preferred_element_type=jnp.float32)))
                return done

            def after(done):
                for c, slot, columns in done:
                    weights[c, slot] = columns.astype(jnp.bfloat16)

            tables(s, before, after)
            return 0

        lax.fori_loop(1, visits - 1, visit, 0)

    tables(0, lambda _: None, lambda _: None)
    each_group(with_operators)
    tables(visits - 1, lambda _: None, lambda _: None)


def add_visits(start, visiting, table, first_visit, c):
    for i, block in enumerate(visiting):
        term = jnp.dot(block[...], table[c, first_visit + i], preferred_element_type=jnp.float32)
        start = term if start is None else start + term
    return start


def gather_early(*refs):
    *visiting, table, early = refs
    for c in range(table.shape[0]):
        early[c] = add_visits(None, visiting, table, 0, c)


def field_of(weights, combined, slot):
    field = None
    for c in range(weights.shape[0]):
        term = jnp.dot(weights[c, slot], combined[c], preferred_element_type=jnp.float32)
        field = term if field is None else field + term
    return field


def interact_far(early_visits, slots, *refs):
    early, *visiting, table, weights, combined = refs[: len(refs) - len(slots)]
    mixed = []
    for c in range(table.shape[0]):
        mixed.append(add_visits(early[c], visiting, table, early_visits, c).astype(jnp.bfloat16))
        combined[c] = mixed[c]
    for slot, out in zip(slots, refs[len(refs) - len(slots) :]):
        out[...] = field_of(weights, mixed, slot).astype(out.dtype)


def interact_near(slots, weights, combined, *outs):
    for slot, out in zip(slots, outs):
        out[...] = field_of(weights, combined, slot).astype(out.dtype)


def local(source, operators, mie_factor, pair_source, pair_class, pair_scale):
    rows, spheres = source.shape
    classes, full, _ = operators.shape
    visits = pair_source.shape[0]
    groups = full // rows
    blocks = lax.axis_size("blk")
    visiting = [source]
    for s in range(1, visits):
        visiting.append(lax.ppermute(source, "blk", [(b, (b + s) % blocks) for b in range(blocks)]))

    units = (pair_scale.astype(jnp.float32) * SCALE_UNIT).astype(jnp.int32)
    codes = (pair_class * 2**SPHERE_BITS + pair_source) * 2**SCALE_BITS + units
    table, weights = pl.pallas_call(
        prepare,
        out_shape=(
            jax.ShapeDtypeStruct((classes, visits, spheres, spheres), jnp.bfloat16),
            jax.ShapeDtypeStruct((classes, groups, rows, rows), jnp.bfloat16),
        ),
        in_specs=[VMEM, pl.BlockSpec(memory_space=pl.ANY)],
        out_specs=(VMEM, VMEM),
        scratch_shapes=[
            pltpu.VMEM((classes, full, full), jnp.bfloat16),
            pltpu.SemaphoreType.DMA((classes,)),
        ],
        compiler_params=pltpu.CompilerParams(vmem_limit_bytes=40 * 2**20),
        cost_estimate=pl.CostEstimate(
            flops=2 * classes * full * full * rows, bytes_accessed=2 * operators.size, transcendentals=0
        ),
        name="prepare",
    )(codes, operators)

    def call(kernel, out_shape, flops, *operands):
        return pl.pallas_call(
            kernel,
            out_shape=out_shape,
            in_specs=[VMEM] * len(operands),
            out_specs=jax.tree.map(lambda _: VMEM, out_shape),
            compiler_params=pltpu.CompilerParams(vmem_limit_bytes=16 * 2**20),
            cost_estimate=pl.CostEstimate(flops=flops, bytes_accessed=2 * source.size, transcendentals=0),
        )(*operands)

    def shape(dtype, *lead):
        return jax.ShapeDtypeStruct((*lead, rows, spheres), dtype)

    gather = 2 * rows * spheres * spheres * classes
    product = 2 * rows * rows * spheres * classes
    late = max(visits - EARLY, 0)
    early = call(gather_early, shape(jnp.float32, classes), (visits - late) * gather, *visiting[:EARLY], table)
    far, near = (3, 2), (1, 0)
    combined, *sent = call(
        functools.partial(interact_far, EARLY, far),
        (shape(jnp.bfloat16, classes),) + (shape(jnp.bfloat16),) * len(far),
        late * gather + len(far) * product,
        early,
        *visiting[EARLY:],
        table,
        weights,
    )
    others = []
    for d, x in zip(far, sent):
        others.append(lax.ppermute(x, "deg", [(i, i ^ d) for i in range(groups)]))
    sent, field = call(
        functools.partial(interact_near, near),
        (shape(jnp.bfloat16), shape(jnp.float32)),
        len(near) * product,
        weights,
        combined,
    )
    others.append(lax.ppermute(sent, "deg", [(i, i ^ 1) for i in range(groups)]))
    for other in others:
        field = field + other.astype(jnp.float32)
    return source.astype(jnp.float32) - mie_factor * field


def solution(mesh):
    return jax.shard_map(
        local,
        mesh=mesh,
        in_specs=(
            P("deg", "blk"),
            P(),
            P("deg", "blk"),
            P(None, None, "blk"),
            P(None, None, "blk"),
            P(None, None, "blk"),
        ),
        out_specs=P("deg", "blk"),
        check_vma=False,
    )
```

time: 45.2 us -> 32.1 us (0.71)
  Pallas kernels: 16 us -> 8.87 us
  local copies, waits for them, and re-layouts: 6.71 us -> 0.01 us
  other arithmetic: 0.74 us -> 1.53 us
    pallas_call x1, Pallas kernels: 13 us -> 5.5 us  [local(): pl.pallas_call(prepare, out_shape=(jax.ShapeDtypeStruct((classes, visits,...]
    unnamed x12 -> x4, local copies, waits for them, and re-layouts: 6.71 us -> 0.01 us
    add x0 -> x1, other arithmetic: none -> 0.79 us  [local(): (pair_class * 2 ** SPHERE_BITS + pair_source) * 2 ** SCALE_BITS + units]
    pallas_call x1 -> x3, Pallas kernels: 2.99 us -> 3.37 us  [call(): pl.pallas_call(kernel, out_shape=out_shape, in_specs=[VMEM] * len(operand...]
  transfers between devices with their start and end apart: 8 -> 8, of which waited for: 2 -> 2; matrix products, arithmetic and copies ran while one was open for 0% -> 2% of each run, Pallas kernels for 29% -> 21%
where the time goes in v2:
time: 32.1 us; the launch traced here: 31.7 us
  starting transfers between devices  16.7 us (52%)
  Pallas kernels  8.87 us (28%)
  waiting for transfers between devices  4.53 us (14%)
  other arithmetic  1.53 us (5%)
    ppermute x5, starting transfers between devices, local(): lax.ppermute(source, 'blk', [(b, (b + s) % blocks) for b in range(blocks)])  13.1 us
    pallas_call x1, Pallas kernels, local(): pl.pallas_call(prepare, out_shape=(jax.ShapeDtypeStruct((classes, visits,...  5.5 us
    ppermute x2, waiting for transfers between devices, local(): others.append(lax.ppermute(x, 'deg', [(i, i ^ d) for i in range(groups)]))  4.51 us
    pallas_call x3, Pallas kernels, call(): pl.pallas_call(kernel, out_shape=out_shape, in_specs=[VMEM] * len(operand...  3.37 us
    ppermute x1, starting transfers between devices, local(): lax.ppermute(sent, 'deg', [(i, i ^ 1) for i in range(groups)])  2.11 us
    ppermute x2, starting transfers between devices, local(): others.append(lax.ppermute(x, 'deg', [(i, i ^ d) for i in range(groups)]))  1.45 us
    add x1, other arithmetic, local(): (pair_class * 2 ** SPHERE_BITS + pair_source) * 2 ** SCALE_BITS + units  0.79 us
    sub x1, other arithmetic, local(): return source.astype(jnp.float32) - mie_factor * field  0.74 us
  transfers between devices with their start and end apart: 8, of which 2 were waited for; matrix products, arithmetic and copies ran while one was open for 2% of the time, Pallas kernels for 21%

profile of v2, /device:TPU:69, one launch (start us, length us, event | category | flops | bytes accessed | tf_op | source)
XLA Modules:
  0.0 31.7 jit_solution(15139622921468977532)
XLA Ops:
  0.0 0.0 copy-start
  0.0 2.9 %collective-permute-start.2 = (bf16[168,256]{1,0:T(8,128)(2,1)}, bf16[168,256]{1,0:T(8,128)(2,1)S(1)}, u32[]{:S(2)}, u32[]{:S(2)}) collective-permute-start(bf16[168,256]{1,0:T(8,128)(2,1)} %refs_0_.1), channel_id=1, source_target_pairs={{0,12},{4,16},{8,20},{12,24},{16,28},{20,32},{24,36},{28,40},{32,4... | collective-permute-start | bytes 258056 | tf_op jit(solution)/shard_map/ppermute | solution.py:150
  2.9 2.5 %collective-permute-start.1 = (bf16[168,256]{1,0:T(8,128)(2,1)}, bf16[168,256]{1,0:T(8,128)(2,1)S(1)}, u32[]{:S(2)}, u32[]{:S(2)}) collective-permute-start(bf16[168,256]{1,0:T(8,128)(2,1)} %refs_0_.1), channel_id=1, source_target_pairs={{0,8},{4,12},{8,16},{12,20},{16,24},{20,28},{24,32},{28,36},{32,40... | collective-permute-start | bytes 258056 | tf_op jit(solution)/shard_map/ppermute | solution.py:150
  5.3 0.7 %collective-permute-start = (bf16[168,256]{1,0:T(8,128)(2,1)}, bf16[168,256]{1,0:T(8,128)(2,1)S(1)}, u32[]{:S(2)}, u32[]{:S(2)}) collective-permute-start(bf16[168,256]{1,0:T(8,128)(2,1)} %refs_0_.1), channel_id=1, source_target_pairs={{0,4},{4,8},{8,12},{12,16},{16,20},{20,24},{24,28},{28,32},{32,36}... | collective-permute-start | bytes 258056 | tf_op jit(solution)/shard_map/ppermute | solution.py:150
  6.1 4.4 %collective-permute-start.4 = (bf16[168,256]{1,0:T(8,128)(2,1)}, bf16[168,256]{1,0:T(8,128)(2,1)S(1)}, u32[]{:S(2)}, u32[]{:S(2)}) collective-permute-start(bf16[168,256]{1,0:T(8,128)(2,1)} %refs_0_.1), channel_id=1, source_target_pairs={{0,20},{4,24},{8,28},{12,32},{16,36},{20,40},{24,44},{28,48},{32,5... | collective-permute-start | bytes 258056 | tf_op jit(solution)/shard_map/ppermute | solution.py:150
  10.5 2.6 %collective-permute-start.3 = (bf16[168,256]{1,0:T(8,128)(2,1)}, bf16[168,256]{1,0:T(8,128)(2,1)S(1)}, u32[]{:S(2)}, u32[]{:S(2)}) collective-permute-start(bf16[168,256]{1,0:T(8,128)(2,1)} %refs_0_.1), channel_id=1, source_target_pairs={{0,16},{4,20},{8,24},{12,28},{16,32},{20,36},{24,40},{28,44},{32,4... | collective-permute-start | bytes 258056 | tf_op jit(solution)/shard_map/ppermute | solution.py:150
  13.1 0.8 %convert_add_fusion.codes = s32[6,4,256]{2,1,0:T(4,128)S(1)} fusion(bf16[6,4,256]{2,1,0:T(4,128)(2,1)} %param.11, s32[6,4,256]{2,1,0:T(4,128)} %param.9, s32[6,4,256]{2,1,0:T(4,128)} %param.10), kind=kLoop, calls=%fused_computation.1 | loop fusion | flops 43008 | bytes 86016 | tf_op jit(solution)/shard_map/add | solution.py:153
  13.9 5.5 %prepare.1 = (bf16[12,6,256,256]{3,2,1,0:T(8,128)(2,1)S(1)}, bf16[12,4,168,168]{3,2,1,0:T(8,128)(2,1)S(1)}) custom-call(s32[6,4,256]{2,1,0:T(4,128)S(1)} %convert_add_fusion.codes, bf16[12,672,672]{2,1,0:T(8,128)(2,1)} %operators.1), custom_call_target="tpu_custom_call" | custom-call | flops 1820786688 | bytes 10838016 | tf_op jit(solution)/shard_map/prepare/pallas_call | solution.py:154
  19.4 0.0 collective-permute-done.2.refs_3_
  19.4 0.0 collective-permute-done.1.refs_2_
  19.4 0.0 collective-permute-done.refs_1_
  19.5 0.0 copy-done
  19.5 1.3 %shard_map.64.refs_0_ = f32[12,168,256]{2,1,0:T(8,128)S(1)} custom-call(bf16[168,256]{1,0:T(8,128)(2,1)S(1)} %copy-done, bf16[168,256]{1,0:T(8,128)(2,1)S(1)} %collective-permute-done.refs_1_, bf16[168,256]{1,0:T(8,128)(2,1)S(1)} %collective-permute-done.1.refs_2_, bf16[168,256]{1,0:T(8,128)(2,1)S(1)} %collective-permute-done.2.refs_3_, ...), custom_call_target="tpu_custom_call" | custom-call | flops 1056964608 | bytes 86016 | tf_op jit(solution)/shard_map/pallas_call | solution.py:174
  20.8 0.0 collective-permute-done.4.refs_2_
  20.8 0.0 collective-permute-done.3.refs_1_
  20.8 0.0 copy-start.1
  20.8 1.4 %shard_map.65 = (bf16[12,168,256]{2,1,0:T(8,128)(2,1)S(1)}, bf16[168,256]{1,0:T(8,128)(2,1)S(1)}, bf16[168,256]{1,0:T(8,128)(2,1)S(1)}) custom-call(f32[12,168,256]{2,1,0:T(8,128)S(1)} %shard_map.64.refs_0_, bf16[168,256]{1,0:T(8,128)(2,1)S(1)} %collective-permute-done.3.refs_1_, bf16[168,256]{1,0:T(8,128)(2,1)S(1)} %collective-permute-done.4.refs_2_, ...), custom_call_target="tpu_custom_call" | custom-call | flops 875298816 | bytes 86016 | tf_op jit(solution)/shard_map/pallas_call | solution.py:174
  22.2 0.7 %shard_map.66 = (bf16[168,256]{1,0:T(8,128)(2,1)S(1)}, f32[168,256]{1,0:T(8,128)S(1)}) custom-call(bf16[12,4,168,168]{3,2,1,0:T(8,128)(2,1)S(1)} %get-tuple-element.12.refs_4_.weights, bf16[12,168,256]{2,1,0:T(8,128)(2,1)S(1)} %get-tuple-element.14.combined), custom_call_target="tpu_custom_call" | custom-call | flops 346816512 | bytes 86016 | tf_op jit(solution)/shard_map/pallas_call | solution.py:174
  22.9 2.1 %collective-permute-start.7 = (bf16[168,256]{1,0:T(8,128)(2,1)S(1)}, bf16[168,256]{1,0:T(8,128)(2,1)S(1)}, u32[]{:S(2)}, u32[]{:S(2)}) collective-permute-start(bf16[168,256]{1,0:T(8,128)(2,1)S(1)} %get-tuple-element.18), channel_id=1, source_target_pairs={{0,1},{1,0},{2,3},{3,2},{4,5},{5,4},{6,7},{7,6},{8,9},{9,8},{10,11... | collective-permute-start | bytes 258056 | tf_op jit(solution)/shard_map/ppermute | solution.py:210
  25.0 1.4 %collective-permute-start.5 = (bf16[168,256]{1,0:T(8,128)(2,1)S(1)}, bf16[168,256]{1,0:T(8,128)(2,1)S(1)}, u32[]{:S(2)}, u32[]{:S(2)}) collective-permute-start(bf16[168,256]{1,0:T(8,128)(2,1)S(1)} %get-tuple-element.16), channel_id=1, source_target_pairs={{0,3},{1,2},{2,1},{3,0},{4,7},{5,6},{6,5},{7,4},{8,11},{9,10},{10,... | collective-permute-start | bytes 258056 | tf_op jit(solution)/shard_map/ppermute | solution.py:202
  26.4 0.0 collective-permute-start.6
  26.5 0.0 collective-permute-done.7
  26.5 3.2 %collective-permute-done.5 = bf16[168,256]{1,0:T(8,128)(2,1)S(1)} collective-permute-done((bf16[168,256]{1,0:T(8,128)(2,1)S(1)}, bf16[168,256]{1,0:T(8,128)(2,1)S(1)}, u32[]{:S(2)}, u32[]{:S(2)}) %collective-permute-start.5) | collective-permute-done | bytes 86048 | tf_op jit(solution)/shard_map/ppermute | solution.py:202
  29.7 1.3 %collective-permute-done.6 = bf16[168,256]{1,0:T(8,128)(2,1)S(1)} collective-permute-done((bf16[168,256]{1,0:T(8,128)(2,1)S(1)}, bf16[168,256]{1,0:T(8,128)(2,1)S(1)}, u32[]{:S(2)}, u32[]{:S(2)}) %collective-permute-start.6) | collective-permute-done | bytes 86048 | tf_op jit(solution)/shard_map/ppermute | solution.py:202
  31.0 0.0 copy-done.1
  31.0 0.7 %multiply_subtract_fusion = f32[168,256]{1,0:T(8,128)} fusion(f32[168,256]{1,0:T(8,128)S(1)} %copy-done.1, bf16[168,256]{1,0:T(8,128)(2,1)S(1)} %collective-permute-done.7, bf16[168,256]{1,0:T(8,128)(2,1)S(1)} %collective-permute-done.6, f32[168,256]{1,0:T(8,128)S(1)} %get-tuple-element.15, bf16[168,256]{1,0:T(8,128)(2,1)S(1)} %collective-permute-done.5, ...), kind=kLoop, calls=%fused_computation | loop fusion | flops 387072 | bytes 860160 | tf_op jit(solution)/shard_map/sub | solution.py:213
Async XLA Ops:
  0.0 19.5 %copy-start = (bf16[168,256]{1,0:T(8,128)(2,1)S(1)}, bf16[168,256]{1,0:T(8,128)(2,1)}, u32[]{:S(2)}) copy-start(bf16[168,256]{1,0:T(8,128)(2,1)} %refs_0_.1) | copy-start | bytes 258052
  0.0 19.4 %collective-permute-start.2 = (bf16[168,256]{1,0:T(8,128)(2,1)}, bf16[168,256]{1,0:T(8,128)(2,1)S(1)}, u32[]{:S(2)}, u32[]{:S(2)}) collective-permute-start(bf16[168,256]{1,0:T(8,128)(2,1)} %refs_0_.1), channel_id=1, source_target_pairs={{0,12},{4,16},{8,20},{12,24},{16,28},{20,32},{24,36},{28,40},{32,4... | collective-permute-start | bytes 258056 | tf_op jit(solution)/shard_map/ppermute | solution.py:150
  2.9 16.6 %collective-permute-start.1 = (bf16[168,256]{1,0:T(8,128)(2,1)}, bf16[168,256]{1,0:T(8,128)(2,1)S(1)}, u32[]{:S(2)}, u32[]{:S(2)}) collective-permute-start(bf16[168,256]{1,0:T(8,128)(2,1)} %refs_0_.1), channel_id=1, source_target_pairs={{0,8},{4,12},{8,16},{12,20},{16,24},{20,28},{24,32},{28,36},{32,40... | collective-permute-start | bytes 258056 | tf_op jit(solution)/shard_map/ppermute | solution.py:150
  5.3 14.1 %collective-permute-start = (bf16[168,256]{1,0:T(8,128)(2,1)}, bf16[168,256]{1,0:T(8,128)(2,1)S(1)}, u32[]{:S(2)}, u32[]{:S(2)}) collective-permute-start(bf16[168,256]{1,0:T(8,128)(2,1)} %refs_0_.1), channel_id=1, source_target_pairs={{0,4},{4,8},{8,12},{12,16},{16,20},{20,24},{24,28},{28,32},{32,36}... | collective-permute-start | bytes 258056 | tf_op jit(solution)/shard_map/ppermute | solution.py:150
  6.1 14.7 %collective-permute-start.4 = (bf16[168,256]{1,0:T(8,128)(2,1)}, bf16[168,256]{1,0:T(8,128)(2,1)S(1)}, u32[]{:S(2)}, u32[]{:S(2)}) collective-permute-start(bf16[168,256]{1,0:T(8,128)(2,1)} %refs_0_.1), channel_id=1, source_target_pairs={{0,20},{4,24},{8,28},{12,32},{16,36},{20,40},{24,44},{28,48},{32,5... | collective-permute-start | bytes 258056 | tf_op jit(solution)/shard_map/ppermute | solution.py:150
  10.5 10.3 %collective-permute-start.3 = (bf16[168,256]{1,0:T(8,128)(2,1)}, bf16[168,256]{1,0:T(8,128)(2,1)S(1)}, u32[]{:S(2)}, u32[]{:S(2)}) collective-permute-start(bf16[168,256]{1,0:T(8,128)(2,1)} %refs_0_.1), channel_id=1, source_target_pairs={{0,16},{4,20},{8,24},{12,28},{16,32},{20,36},{24,40},{28,44},{32,4... | collective-permute-start | bytes 258056 | tf_op jit(solution)/shard_map/ppermute | solution.py:150
  20.8 10.2 %copy-start.1 = (f32[168,256]{1,0:T(8,128)S(1)}, f32[168,256]{1,0:T(8,128)}, u32[]{:S(2)}) copy-start(f32[168,256]{1,0:T(8,128)} %param.8) | copy-start | bytes 516100
  22.9 3.6 %collective-permute-start.7 = (bf16[168,256]{1,0:T(8,128)(2,1)S(1)}, bf16[168,256]{1,0:T(8,128)(2,1)S(1)}, u32[]{:S(2)}, u32[]{:S(2)}) collective-permute-start(bf16[168,256]{1,0:T(8,128)(2,1)S(1)} %get-tuple-element.18), channel_id=1, source_target_pairs={{0,1},{1,0},{2,3},{3,2},{4,5},{5,4},{6,7},{7,6},{8,9},{9,8},{10,11... | collective-permute-start | bytes 258056 | tf_op jit(solution)/shard_map/ppermute | solution.py:210
  25.0 4.6 %collective-permute-start.5 = (bf16[168,256]{1,0:T(8,128)(2,1)S(1)}, bf16[168,256]{1,0:T(8,128)(2,1)S(1)}, u32[]{:S(2)}, u32[]{:S(2)}) collective-permute-start(bf16[168,256]{1,0:T(8,128)(2,1)S(1)} %get-tuple-element.16), channel_id=1, source_target_pairs={{0,3},{1,2},{2,1},{3,0},{4,7},{5,6},{6,5},{7,4},{8,11},{9,10},{10,... | collective-permute-start | bytes 258056 | tf_op jit(solution)/shard_map/ppermute | solution.py:202
  26.4 4.5 %collective-permute-start.6 = (bf16[168,256]{1,0:T(8,128)(2,1)S(1)}, bf16[168,256]{1,0:T(8,128)(2,1)S(1)}, u32[]{:S(2)}, u32[]{:S(2)}) collective-permute-start(bf16[168,256]{1,0:T(8,128)(2,1)S(1)} %get-tuple-element.17), channel_id=1, source_target_pairs={{0,2},{1,3},{2,0},{3,1},{4,6},{5,7},{6,4},{7,5},{8,10},{9,11},{10,... | collective-permute-start | bytes 258056 | tf_op jit(solution)/shard_map/ppermute | solution.py:202

commit v3 on v2

v3 whole, which is shorter than its diff:
```python
import functools

import jax
import jax.numpy as jnp
from jax import lax
from jax.experimental import pallas as pl
from jax.experimental.pallas import tpu as pltpu
from jax.sharding import PartitionSpec as P


LANES = 128
STRIP = 32
EARLY = 4
SPHERE_BITS = 8
SCALE_BITS = 10
SCALE_UNIT = 512
DEPTH = 256
LEAD = 8
VMEM = pl.BlockSpec(memory_space=pltpu.VMEM)


def column_windows(full, rows):
    windows = []
    for d in range(full // rows):
        start = d * rows // LANES * LANES
        if (d + 1) * rows - start > DEPTH:
            start += LANES
        windows.append((start, min(DEPTH, full - start), d * rows - start))
        assert windows[-1][2] >= -LEAD and windows[-1][2] % 8 == 0
    return windows


def prepare(codes, operators, table, weights, extra, stage, arrived):
    classes, full, _ = operators.shape
    visits, slots, spheres = codes.shape
    rows = full // lax.axis_size("deg")
    deg = lax.axis_index("deg")
    windows = column_windows(full, rows)

    def window(d, c):
        start, length, _ = windows[d]
        if length == DEPTH:
            return pltpu.make_async_copy(operators.at[c, :, start : start + length], weights.at[c], arrived.at[c])
        return pltpu.make_async_copy(operators.at[c], stage.at[c], arrived.at[c])

    def each_group(body):
        for d in range(full // rows):
            pl.when(deg == d)(functools.partial(body, d))

    def fetch(d):
        for c in range(classes):
            window(d, c).start()

    each_group(fetch)

    def spread(x, k):
        return jnp.broadcast_to(x[k : k + 1, :], (STRIP, spheres))

    zero = jnp.zeros((), jnp.bfloat16)
    sphere = lax.broadcasted_iota(jnp.int32, (STRIP, spheres), 0).astype(jnp.float32).astype(jnp.bfloat16)

    def tables(s, _):
        kind = jnp.right_shift(codes[s], SPHERE_BITS + SCALE_BITS)
        picked = jnp.bitwise_and(jnp.right_shift(codes[s], SCALE_BITS), 2**SPHERE_BITS - 1)
        scale = jnp.bitwise_and(codes[s], 2**SCALE_BITS - 1).astype(jnp.float32) * (1.0 / SCALE_UNIT)
        picked, scale = picked.astype(jnp.float32).astype(jnp.bfloat16), scale.astype(jnp.bfloat16)
        picked = [spread(picked, k) for k in range(slots)]
        scale = [spread(scale, k) for k in range(slots)]
        mine = []
        for c in range(classes):
            flags = jnp.where(kind == c, 1.0, 0.0).astype(jnp.bfloat16)
            mine.append([spread(flags, k) for k in range(slots)])
        for start in range(0, spheres, STRIP):
            here = sphere + jnp.asarray(start, jnp.bfloat16)
            hits = [jnp.where(here == picked[k], scale[k], zero) for k in range(slots)]
            for c in range(classes):
                terms = [hits[k] * mine[c][k] for k in range(slots)]
                while len(terms) > 1:
                    terms = [sum(terms[i + 1 : i + 2], terms[i]) for i in range(0, len(terms), 2)]
                table[c, s, start : start + STRIP] = terms[0]
        return 0

    lax.fori_loop(0, visits, tables, 0)

    def finish(d):
        start, length, first_row = windows[d]
        whole = length // LANES * LANES
        row = lax.broadcasted_iota(jnp.int32, (LANES, extra.shape[1]), 0) - (LANES + first_row)
        column = lax.broadcasted_iota(jnp.int32, (LANES, extra.shape[1]), 1)
        before = None
        for c in range(classes):
            window(d, c).wait()
            if length < DEPTH:
                weights[c, :, :whole] = stage[c, :, start : start + whole]
                weights[c, :, whole:] = jnp.zeros((full, DEPTH - whole), jnp.bfloat16)
                weights[c, :, whole:length] = stage[c, :, start + whole : start + length]
            if first_row < 0:
                pick = jnp.where((row >= 0) & (row + LEAD * c == column), 1.0, 0.0).astype(jnp.bfloat16)
                term = jnp.dot(stage[c, :, start - LANES : start], pick, preferred_element_type=jnp.float32)
                before = term if before is None else before + term
        extra[...] = jnp.zeros_like(extra) if before is None else before.astype(jnp.bfloat16)

    each_group(finish)


def add_visits(start, visiting, table, first_visit, c):
    for i, block in enumerate(visiting):
        term = jnp.dot(block[...], table[c, first_visit + i], preferred_element_type=jnp.float32)
        start = term if start is None else start + term
    return start


def gather_early(*refs):
    *visiting, table, early = refs
    for c in range(table.shape[0]):
        early[c] = add_visits(None, visiting, table, 0, c)


def field_of(weights, extra, combined, slot):
    rows = extra.shape[0] // lax.axis_size("deg")
    chunk = pl.ds(pl.multiple_of(jnp.bitwise_xor(lax.axis_index("deg"), slot) * rows, 8), rows)
    lead = jnp.concatenate([combined[c, :LEAD] for c in range(weights.shape[0])], axis=0)
    field = jnp.dot(extra[chunk], lead, preferred_element_type=jnp.float32)
    for c in range(weights.shape[0]):
        field += jnp.dot(weights[c, chunk], combined[c, LEAD:], preferred_element_type=jnp.float32)
    return field


def interact_far(early_visits, slots, *refs):
    early, *visiting, table, weights, extra, combined = refs[: len(refs) - len(slots)]
    rows = early.shape[1]
    place = jnp.int32(LEAD)
    for d, (_, _, first_row) in enumerate(column_windows(weights.shape[1], rows)):
        place += jnp.where(lax.axis_index("deg") == d, first_row, 0)
    combined[...] = jnp.zeros_like(combined)
    for c in range(table.shape[0]):
        mixed = add_visits(early[c], visiting, table, early_visits, c)
        combined[c, pl.ds(pl.multiple_of(place, 8), rows)] = mixed.astype(jnp.bfloat16)
    for slot, out in zip(slots, refs[len(refs) - len(slots) :]):
        out[...] = field_of(weights, extra, combined, slot).astype(out.dtype)


def interact_near(slots, weights, extra, combined, *outs):
    for slot, out in zip(slots, outs):
        out[...] = field_of(weights, extra, combined, slot).astype(out.dtype)


def local(source, operators, mie_factor, pair_source, pair_class, pair_scale):
    rows, spheres = source.shape
    classes, full, _ = operators.shape
    visits = pair_source.shape[0]
    groups = full // rows
    blocks = lax.axis_size("blk")
    visiting = [source]
    for s in range(1, visits):
        visiting.append(lax.ppermute(source, "blk", [(b, (b + s) % blocks) for b in range(blocks)]))

    units = (pair_scale.astype(jnp.float32) * SCALE_UNIT).astype(jnp.int32)
    codes = (pair_class * 2**SPHERE_BITS + pair_source) * 2**SCALE_BITS + units
    table, weights, extra = pl.pallas_call(
        prepare,
        out_shape=(
            jax.ShapeDtypeStruct((classes, visits, spheres, spheres), jnp.bfloat16),
            jax.ShapeDtypeStruct((classes, full, DEPTH), jnp.bfloat16),
            jax.ShapeDtypeStruct((full, LEAD * classes), jnp.bfloat16),
        ),
        in_specs=[VMEM, pl.BlockSpec(memory_space=pl.ANY)],
        out_specs=(VMEM,) * 3,
        scratch_shapes=[
            pltpu.VMEM((classes, full, full), jnp.bfloat16),
            pltpu.SemaphoreType.DMA((classes,)),
        ],
        compiler_params=pltpu.CompilerParams(vmem_limit_bytes=40 * 2**20),
        cost_estimate=pl.CostEstimate(
            flops=2 * classes * full * full * rows, bytes_accessed=2 * operators.size, transcendentals=0
        ),
        name="prepare",
    )(codes, operators)

    def call(kernel, out_shape, flops, *operands):
        return pl.pallas_call(
            kernel,
            out_shape=out_shape,
            in_specs=[VMEM] * len(operands),
            out_specs=jax.tree.map(lambda _: VMEM, out_shape),
            compiler_params=pltpu.CompilerParams(vmem_limit_bytes=16 * 2**20),
            cost_estimate=pl.CostEstimate(flops=flops, bytes_accessed=2 * source.size, transcendentals=0),
        )(*operands)

    def shape(dtype, *lead):
        return jax.ShapeDtypeStruct((*lead, rows, spheres), dtype)

    gather = 2 * rows * spheres * spheres * classes
    product = 2 * rows * rows * spheres * classes
    late = max(visits - EARLY, 0)
    early = call(gather_early, shape(jnp.float32, classes), (visits - late) * gather, *visiting[:EARLY], table)

    def exchange(x, distance):
        return lax.ppermute(x, "deg", [(i, i ^ distance) for i in range(groups)])

    far, near = (3,), (2, 1, 0)
    combined, crossed = call(
        functools.partial(interact_far, EARLY, far),
        (jax.ShapeDtypeStruct((classes, LEAD + DEPTH, spheres), jnp.bfloat16), shape(jnp.bfloat16)),
        late * gather + len(far) * product,
        early,
        *visiting[EARLY:],
        table,
        weights,
        extra,
    )
    crossed = exchange(crossed, 1)
    ahead, beside, field = call(
        functools.partial(interact_near, near),
        (shape(jnp.float32), shape(jnp.bfloat16), shape(jnp.float32)),
        len(near) * product,
        weights,
        extra,
        combined,
    )
    ahead = exchange((ahead + crossed.astype(jnp.float32)).astype(jnp.bfloat16), 2)
    beside = exchange(beside, 1)
    field = field + beside.astype(jnp.float32) + ahead.astype(jnp.float32)
    return source.astype(jnp.float32) - mie_factor * field


def solution(mesh):
    return jax.shard_map(
        local,
        mesh=mesh,
        in_specs=(
            P("deg", "blk"),
            P(),
            P("deg", "blk"),
            P(None, None, "blk"),
            P(None, None, "blk"),
            P(None, None, "blk"),
        ),
        out_specs=P("deg", "blk"),
        check_vma=False,
    )
```

time: 32.1 us -> 29.5 us (0.919)
  waiting for transfers between devices: 4.53 us -> 2.59 us
  Pallas kernels: 8.87 us -> 7.3 us
  starting transfers between devices: 16.7 us -> 17.4 us
    pallas_call x1, Pallas kernels: 5.5 us -> 3.23 us  [local(): pl.pallas_call(prepare, out_shape=(jax.ShapeDtypeStruct((classes, visits,...]
    ppermute x3, waiting for transfers between devices: 4.52 us -> 2.58 us  [exchange(): return lax.ppermute(x, 'deg', [(i, i ^ distance) for i in range(groups)])]
    pallas_call x3, Pallas kernels: 3.37 us -> 4.06 us  [call(): pl.pallas_call(kernel, out_shape=out_shape, in_specs=[VMEM] * len(operand...]
    ppermute x3, starting transfers between devices: 3.56 us -> 4.25 us  [exchange(): return lax.ppermute(x, 'deg', [(i, i ^ distance) for i in range(groups)])]
  transfers between devices with their start and end apart: 8 -> 8, of which waited for: 2 -> 1; matrix products, arithmetic and copies ran while one was open for 2% -> 3% of each run, Pallas kernels for 21% -> 19%
where the time goes in v3:
time: 29.5 us; the launch traced here: 28.9 us
  starting transfers between devices  17.4 us (59%)
  Pallas kernels  7.3 us (25%)
  waiting for transfers between devices  2.59 us (9%)
  other arithmetic  1.54 us (5%)
    ppermute x5, starting transfers between devices, local(): lax.ppermute(source, 'blk', [(b, (b + s) % blocks) for b in range(blocks)])  13.1 us
    ppermute x3, starting transfers between devices, exchange(): return lax.ppermute(x, 'deg', [(i, i ^ distance) for i in range(groups)])  4.25 us
    pallas_call x3, Pallas kernels, call(): pl.pallas_call(kernel, out_shape=out_shape, in_specs=[VMEM] * len(operand...  4.06 us
    pallas_call x1, Pallas kernels, local(): pl.pallas_call(prepare, out_shape=(jax.ShapeDtypeStruct((classes, visits,...  3.23 us
    ppermute x3, waiting for transfers between devices, exchange(): return lax.ppermute(x, 'deg', [(i, i ^ distance) for i in range(groups)])  2.58 us
    add x1, other arithmetic, local(): (pair_class * 2 ** SPHERE_BITS + pair_source) * 2 ** SCALE_BITS + units  0.79 us
    sub x1, other arithmetic, local(): return source.astype(jnp.float32) - mie_factor * field  0.73 us
  transfers between devices with their start and end apart: 8, of which 1 were waited for; matrix products, arithmetic and copies ran while one was open for 3% of the time, Pallas kernels for 19%

profile of v3, /device:TPU:69, one launch (start us, length us, event | category | flops | bytes accessed | tf_op | source)
XLA Modules:
  0.0 28.9 jit_solution(10794463153979218945)
XLA Ops:
  0.0 2.9 %collective-permute-start.2 = (bf16[168,256]{1,0:T(8,128)(2,1)}, bf16[168,256]{1,0:T(8,128)(2,1)S(1)}, u32[]{:S(2)}, u32[]{:S(2)}) collective-permute-start(bf16[168,256]{1,0:T(8,128)(2,1)} %refs_0_.1), channel_id=1, source_target_pairs={{0,12},{4,16},{8,20},{12,24},{16,28},{20,32},{24,36},{28,40},{32,4... | collective-permute-start | bytes 258056 | tf_op jit(solution)/shard_map/ppermute | solution.py:156
  2.9 2.5 %collective-permute-start.1 = (bf16[168,256]{1,0:T(8,128)(2,1)}, bf16[168,256]{1,0:T(8,128)(2,1)S(1)}, u32[]{:S(2)}, u32[]{:S(2)}) collective-permute-start(bf16[168,256]{1,0:T(8,128)(2,1)} %refs_0_.1), channel_id=1, source_target_pairs={{0,8},{4,12},{8,16},{12,20},{16,24},{20,28},{24,32},{28,36},{32,40... | collective-permute-start | bytes 258056 | tf_op jit(solution)/shard_map/ppermute | solution.py:156
  5.3 0.7 %collective-permute-start = (bf16[168,256]{1,0:T(8,128)(2,1)}, bf16[168,256]{1,0:T(8,128)(2,1)S(1)}, u32[]{:S(2)}, u32[]{:S(2)}) collective-permute-start(bf16[168,256]{1,0:T(8,128)(2,1)} %refs_0_.1), channel_id=1, source_target_pairs={{0,4},{4,8},{8,12},{12,16},{16,20},{20,24},{24,28},{28,32},{32,36}... | collective-permute-start | bytes 258056 | tf_op jit(solution)/shard_map/ppermute | solution.py:156
  6.1 4.4 %collective-permute-start.4 = (bf16[168,256]{1,0:T(8,128)(2,1)}, bf16[168,256]{1,0:T(8,128)(2,1)S(1)}, u32[]{:S(2)}, u32[]{:S(2)}) collective-permute-start(bf16[168,256]{1,0:T(8,128)(2,1)} %refs_0_.1), channel_id=1, source_target_pairs={{0,20},{4,24},{8,28},{12,32},{16,36},{20,40},{24,44},{28,48},{32,5... | collective-permute-start | bytes 258056 | tf_op jit(solution)/shard_map/ppermute | solution.py:156
  10.5 2.6 %collective-permute-start.3 = (bf16[168,256]{1,0:T(8,128)(2,1)}, bf16[168,256]{1,0:T(8,128)(2,1)S(1)}, u32[]{:S(2)}, u32[]{:S(2)}) collective-permute-start(bf16[168,256]{1,0:T(8,128)(2,1)} %refs_0_.1), channel_id=1, source_target_pairs={{0,16},{4,20},{8,24},{12,28},{16,32},{20,36},{24,40},{28,44},{32,4... | collective-permute-start | bytes 258056 | tf_op jit(solution)/shard_map/ppermute | solution.py:156
  13.1 0.8 %convert_add_fusion.codes = s32[6,4,256]{2,1,0:T(4,128)S(1)} fusion(bf16[6,4,256]{2,1,0:T(4,128)(2,1)} %param.11, s32[6,4,256]{2,1,0:T(4,128)} %param.9, s32[6,4,256]{2,1,0:T(4,128)} %param.10), kind=kLoop, calls=%fused_computation.2 | loop fusion | flops 43008 | bytes 86016 | tf_op jit(solution)/shard_map/add | solution.py:159
  13.9 0.0 copy-start
  13.9 3.2 %prepare.1 = (bf16[12,6,256,256]{3,2,1,0:T(8,128)(2,1)S(1)}, bf16[12,672,256]{2,1,0:T(8,128)(2,1)S(1)}, bf16[672,96]{1,0:T(8,128)(2,1)S(1)}) custom-call(s32[6,4,256]{2,1,0:T(4,128)S(1)} %convert_add_fusion.codes, bf16[12,672,672]{2,1,0:T(8,128)(2,1)} %operators.1), custom_call_target="tpu_custom_call" | custom-call | flops 1820786688 | bytes 10838016 | tf_op jit(solution)/shard_map/prepare/pallas_call | solution.py:160
  17.2 0.0 collective-permute-done.2.refs_3_
  17.2 0.0 collective-permute-done.1.refs_2_
  17.2 0.0 collective-permute-done.refs_1_
  17.2 0.0 copy-done
  17.2 1.3 %shard_map.64.refs_0_ = f32[12,168,256]{2,1,0:T(8,128)S(1)} custom-call(bf16[168,256]{1,0:T(8,128)(2,1)S(1)} %copy-done, bf16[168,256]{1,0:T(8,128)(2,1)S(1)} %collective-permute-done.refs_1_, bf16[168,256]{1,0:T(8,128)(2,1)S(1)} %collective-permute-done.1.refs_2_, bf16[168,256]{1,0:T(8,128)(2,1)S(1)} %collective-permute-done.2.refs_3_, ...), custom_call_target="tpu_custom_call" | custom-call | flops 1056964608 | bytes 86016 | tf_op jit(solution)/shard_map/pallas_call | solution.py:181
  18.5 0.0 collective-permute-done.4.refs_2_
  18.5 0.0 collective-permute-done.3.refs_1_
  18.5 1.7 %shard_map.65 = (bf16[12,264,256]{2,1,0:T(8,128)(2,1)S(1)}, bf16[168,256]{1,0:T(8,128)(2,1)S(1)}) custom-call(f32[12,168,256]{2,1,0:T(8,128)S(1)} %shard_map.64.refs_0_, bf16[168,256]{1,0:T(8,128)(2,1)S(1)} %collective-permute-done.3.refs_1_, bf16[168,256]{1,0:T(8,128)(2,1)S(1)} %collective-permute-done.4.refs_2_, ...), custom_call_target="tpu_custom_call" | custom-call | flops 701890560 | bytes 86016 | tf_op jit(solution)/shard_map/pallas_call | solution.py:181
  20.3 0.0 copy-start.1
  20.3 2.2 %collective-permute-start.6 = (bf16[168,256]{1,0:T(8,128)(2,1)S(1)}, bf16[168,256]{1,0:T(8,128)(2,1)S(1)}, u32[]{:S(2)}, u32[]{:S(2)}) collective-permute-start(bf16[168,256]{1,0:T(8,128)(2,1)S(1)} %get-tuple-element.20), channel_id=1, source_target_pairs={{0,1},{1,0},{2,3},{3,2},{4,5},{5,4},{6,7},{7,6},{8,9},{9,8},{10,11... | collective-permute-start | bytes 258056 | tf_op jit(solution)/shard_map/ppermute | solution.py:199
  22.4 1.1 %shard_map.66 = (f32[168,256]{1,0:T(8,128)S(1)}, bf16[168,256]{1,0:T(8,128)(2,1)S(1)}, f32[168,256]{1,0:T(8,128)S(1)}) custom-call(bf16[12,672,256]{2,1,0:T(8,128)(2,1)S(1)} %get-tuple-element.13.refs_4_.weights, bf16[672,96]{1,0:T(8,128)(2,1)S(1)} %get-tuple-element.14.refs_5_.extra, bf16[12,264,256]{2,1,0:T(8,128)(2,1)S(1)} %get-tuple-element.16.combined), custom_call_target="tpu_custom_call" | custom-call | flops 520224768 | bytes 86016 | tf_op jit(solution)/shard_map/pallas_call | solution.py:181
  23.5 0.1 collective-permute-start.5
  23.6 0.0 collective-permute-done.6
  23.6 2.0 %collective-permute-start.7 = (bf16[168,256]{1,0:T(8,128)(2,1)S(1)}, bf16[168,256]{1,0:T(8,128)(2,1)S(1)}, u32[]{:S(2)}, u32[]{:S(2)}) collective-permute-start(bf16[168,256]{1,0:T(8,128)(2,1)S(1)} %add_convert_fusion), channel_id=1, source_target_pairs={{0,2},{1,3},{2,0},{3,1},{4,6},{5,7},{6,4},{7,5},{8,10},{9,11},{10,... | collective-permute-start | bytes 258056 | tf_op jit(solution)/shard_map/ppermute | solution.py:199
  25.6 0.0 collective-permute-done.5
  25.6 2.6 %collective-permute-done.7 = bf16[168,256]{1,0:T(8,128)(2,1)S(1)} collective-permute-done((bf16[168,256]{1,0:T(8,128)(2,1)S(1)}, bf16[168,256]{1,0:T(8,128)(2,1)S(1)}, u32[]{:S(2)}, u32[]{:S(2)}) %collective-permute-start.7) | collective-permute-done | bytes 86048 | tf_op jit(solution)/shard_map/ppermute | solution.py:199
  28.2 0.0 copy-done.1
  28.2 0.7 %multiply_subtract_fusion = f32[168,256]{1,0:T(8,128)} fusion(f32[168,256]{1,0:T(8,128)S(1)} %copy-done.1, bf16[168,256]{1,0:T(8,128)(2,1)S(1)} %collective-permute-done.7, f32[168,256]{1,0:T(8,128)S(1)} %get-tuple-element.17, bf16[168,256]{1,0:T(8,128)(2,1)S(1)} %collective-permute-done.5, bf16[168,256]{1,0:T(8,128)(2,1)S(1)} %copy-done), kind=kLoop, calls=%fused_computation | loop fusion | flops 301056 | bytes 774144 | tf_op jit(solution)/shard_map/sub | solution.py:224
  (1 shorter events, 0.0 us)
Async XLA Ops:
  0.0 17.2 %collective-permute-start.2 = (bf16[168,256]{1,0:T(8,128)(2,1)}, bf16[168,256]{1,0:T(8,128)(2,1)S(1)}, u32[]{:S(2)}, u32[]{:S(2)}) collective-permute-start(bf16[168,256]{1,0:T(8,128)(2,1)} %refs_0_.1), channel_id=1, source_target_pairs={{0,12},{4,16},{8,20},{12,24},{16,28},{20,32},{24,36},{28,40},{32,4... | collective-permute-start | bytes 258056 | tf_op jit(solution)/shard_map/ppermute | solution.py:156
  2.9 14.3 %collective-permute-start.1 = (bf16[168,256]{1,0:T(8,128)(2,1)}, bf16[168,256]{1,0:T(8,128)(2,1)S(1)}, u32[]{:S(2)}, u32[]{:S(2)}) collective-permute-start(bf16[168,256]{1,0:T(8,128)(2,1)} %refs_0_.1), channel_id=1, source_target_pairs={{0,8},{4,12},{8,16},{12,20},{16,24},{20,28},{24,32},{28,36},{32,40... | collective-permute-start | bytes 258056 | tf_op jit(solution)/shard_map/ppermute | solution.py:156
  5.3 11.9 %collective-permute-start = (bf16[168,256]{1,0:T(8,128)(2,1)}, bf16[168,256]{1,0:T(8,128)(2,1)S(1)}, u32[]{:S(2)}, u32[]{:S(2)}) collective-permute-start(bf16[168,256]{1,0:T(8,128)(2,1)} %refs_0_.1), channel_id=1, source_target_pairs={{0,4},{4,8},{8,12},{12,16},{16,20},{20,24},{24,28},{28,32},{32,36}... | collective-permute-start | bytes 258056 | tf_op jit(solution)/shard_map/ppermute | solution.py:156
  6.1 12.5 %collective-permute-start.4 = (bf16[168,256]{1,0:T(8,128)(2,1)}, bf16[168,256]{1,0:T(8,128)(2,1)S(1)}, u32[]{:S(2)}, u32[]{:S(2)}) collective-permute-start(bf16[168,256]{1,0:T(8,128)(2,1)} %refs_0_.1), channel_id=1, source_target_pairs={{0,20},{4,24},{8,28},{12,32},{16,36},{20,40},{24,44},{28,48},{32,5... | collective-permute-start | bytes 258056 | tf_op jit(solution)/shard_map/ppermute | solution.py:156
  10.5 8.0 %collective-permute-start.3 = (bf16[168,256]{1,0:T(8,128)(2,1)}, bf16[168,256]{1,0:T(8,128)(2,1)S(1)}, u32[]{:S(2)}, u32[]{:S(2)}) collective-permute-start(bf16[168,256]{1,0:T(8,128)(2,1)} %refs_0_.1), channel_id=1, source_target_pairs={{0,16},{4,20},{8,24},{12,28},{16,32},{20,36},{24,40},{28,44},{32,4... | collective-permute-start | bytes 258056 | tf_op jit(solution)/shard_map/ppermute | solution.py:156
  13.9 3.3 %copy-start = (bf16[168,256]{1,0:T(8,128)(2,1)S(1)}, bf16[168,256]{1,0:T(8,128)(2,1)}, u32[]{:S(2)}) copy-start(bf16[168,256]{1,0:T(8,128)(2,1)} %refs_0_.1) | copy-start | bytes 258052
  20.3 7.9 %copy-start.1 = (f32[168,256]{1,0:T(8,128)S(1)}, f32[168,256]{1,0:T(8,128)}, u32[]{:S(2)}) copy-start(f32[168,256]{1,0:T(8,128)} %param.8) | copy-start | bytes 516100
  20.3 3.3 %collective-permute-start.6 = (bf16[168,256]{1,0:T(8,128)(2,1)S(1)}, bf16[168,256]{1,0:T(8,128)(2,1)S(1)}, u32[]{:S(2)}, u32[]{:S(2)}) collective-permute-start(bf16[168,256]{1,0:T(8,128)(2,1)S(1)} %get-tuple-element.20), channel_id=1, source_target_pairs={{0,1},{1,0},{2,3},{3,2},{4,5},{5,4},{6,7},{7,6},{8,9},{9,8},{10,11... | collective-permute-start | bytes 258056 | tf_op jit(solution)/shard_map/ppermute | solution.py:199
  23.5 2.1 %collective-permute-start.5 = (bf16[168,256]{1,0:T(8,128)(2,1)S(1)}, bf16[168,256]{1,0:T(8,128)(2,1)S(1)}, u32[]{:S(2)}, u32[]{:S(2)}) collective-permute-start(bf16[168,256]{1,0:T(8,128)(2,1)S(1)} %get-tuple-element.18), channel_id=1, source_target_pairs={{0,1},{1,0},{2,3},{3,2},{4,5},{5,4},{6,7},{7,6},{8,9},{9,8},{10,11... | collective-permute-start | bytes 258056 | tf_op jit(solution)/shard_map/ppermute | solution.py:199
  23.6 4.6 %collective-permute-start.7 = (bf16[168,256]{1,0:T(8,128)(2,1)S(1)}, bf16[168,256]{1,0:T(8,128)(2,1)S(1)}, u32[]{:S(2)}, u32[]{:S(2)}) collective-permute-start(bf16[168,256]{1,0:T(8,128)(2,1)S(1)} %add_convert_fusion), channel_id=1, source_target_pairs={{0,2},{1,3},{2,0},{3,1},{4,6},{5,7},{6,4},{7,5},{8,10},{9,11},{10,... | collective-permute-start | bytes 258056 | tf_op jit(solution)/shard_map/ppermute | solution.py:199
